TPU v7x, 32 devices: a whole 2x2x4 slice. The times are simulated.
32 devices in a mesh: grp: 2 (over x), blk: 16 (over z, y, core).
Axes of the slice: x: 2, y: 2, z: 4, core: 2. Of those that a mesh axis runs over, the one named last changes fastest.
Arguments:
- params: bfloat16 [2, 7168, 4096], P('grp', 'blk'), may hold values from -0.0625 to 0.0625
- tracker: bfloat16 [2, 7168, 4096], P('grp', 'blk'), may hold values from -0.29882812 to 0.29882812
- hidden: bfloat16 [256, 7168], P('grp', 'blk'), may hold values from -6 to 6
- target: bfloat16 [256, 4096], P('grp'), may hold values from -6 to 6
Outputs:
- params_next: bfloat16 [2, 7168, 4096], P('grp', 'blk')
- tracker_next: bfloat16 [2, 7168, 4096], P('grp', 'blk')
All inputs are finite; a program needn't handle non-finite values.
Results may differ from a plain program's by a relative error of at most 0.01.
Values may be sent and summed in bfloat16 or wider, within the bound.
A program may use at most 192 MiB of HBM per device.

v0:
```python
import functools

import jax
import jax.numpy as jnp
from jax import lax
from jax.experimental import pallas as pl
from jax.experimental.pallas import tpu as pltpu
from jax.sharding import PartitionSpec as P


step_size = 0.05
MESH = pl.DeviceIdType.MESH


def mix_weights(position, groups):
    def has(spot):
        return ((spot >= 0) & (spot < groups)).astype(jnp.float32)

    def row(spot):
        a, b = has(spot - 1) / 3.0, has(spot + 1) / 3.0
        return a, 1.0 - a - b, b

    here, before, after = row(position), row(position - 1), row(position + 1)
    return {
        -2: here[0] * before[0],
        -1: here[0] * before[1] + here[1] * here[0],
        0: here[1] * here[1] + here[0] * before[2] + here[2] * after[0],
        1: here[2] * after[1] + here[1] * here[2],
        2: here[2] * after[2],
    }


def exchange(value, groups):
    if groups == 2:
        return {(-1, 1): lax.ppermute(value, "grp", [(0, 1), (1, 0)])}
    received = {}
    for offset in (-2, -1, 1, 2):
        pairs = [(i, i - offset) for i in range(groups) if 0 <= i - offset < groups]
        if pairs:
            received[(offset,)] = lax.ppermute(value, "grp", pairs)
    return received


def exchange_uneven(value, groups, n):
    if groups != 2 or n % 2:
        return exchange(value, groups)
    both = ("grp", "blk")
    sides = [(g, b) for g in range(groups) for b in range(0, n, 2)]
    lent = lax.ppermute(value, both, [(g * n + b, g * n + b + 1) for g, b in sides])
    for_even = lax.ppermute(lent, both, [(g * n + b + 1, (1 - g) * n + b) for g, b in sides])
    for_odd = lax.ppermute(value, both, [(g * n + b + 1, (1 - g) * n + b + 1) for g, b in sides])
    return {(-1, 1): for_even + for_odd}


def mixed(own, others, weights):
    total = weights[0] * own.astype(jnp.float32)
    for offsets, value in others.items():
        total = total + sum(weights[o] for o in offsets) * value.astype(jnp.float32)
    return total


PIECES = 4


def residual_kernel(
    z_size, part_ref, target_ref, out_ref, core_in, core_sum, y_in, y_sum, z_in, *sems
):
    (core_s, core_r, y_s, y_r, z_s, z_r, gz_s, gz_r, gy_s, gy_r, gc_s, gc_r) = sems
    me = lax.axis_index("blk")
    c = lax.rem(me, 2)
    y = lax.rem(lax.div(me, 2), 2)
    z = lax.div(me, 4)
    core_peer = z * 4 + y * 2 + (1 - c)
    y_peer = z * 4 + (1 - y) * 2 + c
    z_spots = [lax.rem(z + k, z_size) for k in range(1, z_size)]
    z_peers = [spot * 4 + y * 2 + c for spot in z_spots]
    width = target_ref.shape[-1] // PIECES
    columns = [pl.ds(q * width, width) for q in range(PIECES)]

    barrier = pltpu.get_barrier_semaphore()
    for peer in [core_peer, y_peer, *z_peers]:
        pl.semaphore_signal(barrier, inc=1, device_id={"blk": peer}, device_id_type=MESH)
    pl.semaphore_wait(barrier, z_size + 1)

    def send(src, dst, send_sem, recv_sem, peer):
        copy = pltpu.make_async_remote_copy(
            src_ref=src,
            dst_ref=dst,
            send_sem=send_sem,
            recv_sem=recv_sem,
            device_id={"blk": peer},
            device_id_type=MESH,
        )
        copy.start()
        return copy

    over_core = [
        send(part_ref.at[:, :, 1 - c, :, at], core_in.at[:, :, :, at], core_s.at[q], core_r.at[q], core_peer)
        for q, at in enumerate(columns)
    ]
    over_y = []
    for q, at in enumerate(columns):
        over_core[q].wait_recv()
        core_sum[:, :, :, at] = part_ref[:, :, c, :, at] + core_in[:, :, :, at]
        over_y.append(
            send(core_sum.at[:, 1 - y, :, at], y_in.at[:, :, at], y_s.at[q], y_r.at[q], y_peer)
        )
    over_z = []
    for q, at in enumerate(columns):
        over_y[q].wait_recv()
        y_sum[:, :, at] = core_sum[:, y, :, at] + y_in[:, :, at]
        over_z.append([
            send(y_sum.at[spot, :, at], z_in.at[k, :, at], z_s.at[q, k], z_r.at[q, k], z_peers[k])
            for k, spot in enumerate(z_spots)
        ])
    give_z = []
    for q, at in enumerate(columns):
        total = y_sum[z, :, at] - target_ref[:, at].astype(jnp.float32)
        for k, copy in enumerate(over_z[q]):
            copy.wait_recv()
            total = total + z_in[k, :, at]
        out_ref[z, y, c, :, at] = jnp.tanh(total).astype(jnp.bfloat16)
        mine = out_ref.at[z, y, c, :, at]
        give_z.append([
            send(mine, mine, gz_s.at[q, k], gz_r.at[q, k], peer) for k, peer in enumerate(z_peers)
        ])
    give_y = []
    for q, at in enumerate(columns):
        for copy in give_z[q]:
            copy.wait_recv()
        mine = out_ref.at[:, y, c, :, at]
        give_y.append(send(mine, mine, gy_s.at[q], gy_r.at[q], y_peer))
    give_core = []
    for q, at in enumerate(columns):
        give_y[q].wait_recv()
        mine = out_ref.at[:, :, c, :, at]
        give_core.append(send(mine, mine, gc_s.at[q], gc_r.at[q], core_peer))
    for copy in give_core:
        copy.wait_recv()
    for copy in [*over_core, *over_y, *sum(over_z, []), *sum(give_z, []), *give_y, *give_core]:
        copy.wait_send()


def residual(output, own_target, n, which):
    tokens, width = output.shape
    share, z_size = tokens // n, n // 4
    one = pltpu.SemaphoreType.DMA((PIECES,))
    many = pltpu.SemaphoreType.DMA((PIECES, z_size - 1))
    resid = pl.pallas_call(
        functools.partial(residual_kernel, z_size),
        out_shape=jax.ShapeDtypeStruct((z_size, 2, 2, share, width), jnp.bfloat16),
        in_specs=[pl.BlockSpec(memory_space=pltpu.VMEM)] * 2,
        out_specs=pl.BlockSpec(memory_space=pltpu.VMEM),
        scratch_shapes=[
            pltpu.VMEM((z_size, 2, share, width), jnp.float32),
            pltpu.VMEM((z_size, 2, share, width), jnp.float32),
            pltpu.VMEM((z_size, share, width), jnp.float32),
            pltpu.VMEM((z_size, share, width), jnp.float32),
            pltpu.VMEM((z_size - 1, share, width), jnp.float32),
            one, one, one, one, many, many, many, many, one, one, one, one,
        ],
        compiler_params=pltpu.CompilerParams(collective_id=which, has_side_effects=True),
        cost_estimate=pl.CostEstimate(flops=0, bytes_accessed=100 * tokens * width, transcendentals=0),
        name="residual",
    )(output.reshape(z_size, 2, 2, share, width), own_target)
    return resid.reshape(tokens, width)


def add_kernel(count, weights_ref, base_ref, *refs):
    out_ref = refs[-1]
    total = base_ref[...]
    for i, other in enumerate(refs[:count]):
        total = total + weights_ref[i] * other[...].astype(jnp.float32)
    out_ref[...] = total.astype(out_ref.dtype)


def add_others(base, others, weights, block):
    rows, width = base.shape
    count = others[0].shape[0] // block
    here = pl.BlockSpec((block, width), lambda i: (i, 0))
    return pl.pallas_call(
        functools.partial(add_kernel, len(others)),
        grid=(count,),
        out_shape=jax.ShapeDtypeStruct((rows, width), jnp.bfloat16),
        in_specs=[pl.BlockSpec(memory_space=pltpu.SMEM), here] + [here] * len(others),
        out_specs=here,
        compiler_params=pltpu.CompilerParams(dimension_semantics=("arbitrary",)),
        cost_estimate=pl.CostEstimate(
            flops=4 * count * block * width, bytes_accessed=8 * count * block * width, transcendentals=0
        ),
        name="add_others",
    )(weights, base, *others)


def step(params, tracker, hidden, target):
    groups, n = lax.axis_size("grp"), lax.axis_size("blk")
    weights = mix_weights(lax.axis_index("grp"), groups)
    tokens = hidden.shape[0]
    share = tokens // n
    own_target = lax.dynamic_slice_in_dim(target, lax.axis_index("blk") * share, share, 0)
    params, tracker = params[0], tracker[0]
    rows = params.shape[0]
    block = 16
    first = rows * 5 // 7 // 16 * 16
    ends = sorted({first, max(first, rows - 32), max(first, rows - 8), rows})
    cuts = list(zip([0, *ends[:-1]], ends))
    other_params = exchange(params, groups)
    slices = [tracker[lo:hi] for lo, hi in cuts]
    other_tracker = []
    for piece in slices[:-1]:
        other_tracker.append(exchange(piece, groups))
    other_tracker.append(exchange_uneven(slices[-1], groups, n))
    output_old = jnp.dot(hidden, params, preferred_element_type=jnp.float32)
    resid_old = residual(output_old, own_target, n, 0)
    params_next = (
        mixed(params, other_params, weights) - step_size * tracker.astype(jnp.float32)
    ).astype(jnp.bfloat16)
    output_new = jnp.dot(hidden, params_next, preferred_element_type=jnp.float32)
    resid_new = residual(output_new, own_target, n, 1)
    change = lax.dot_general(
        jnp.concatenate([hidden, -hidden], 0),
        jnp.concatenate([resid_new, resid_old], 0),
        (((0,), (0,)), ((), ())),
        preferred_element_type=jnp.float32,
    )
    base = weights[0] * tracker.astype(jnp.float32) + change / tokens
    late = lax.optimization_barrier([base[lo:hi] for lo, hi in cuts[1:]])
    gains = jnp.stack([sum(weights[o] for o in offsets) for offsets in other_tracker[0]])
    early = list(other_tracker[0].values())
    height = next(size for size in (10 * block, 4 * block, block) if first % size == 0)
    tracker_next = add_others(base, early, gains, height)
    for (lo, _), piece, received in zip(cuts[1:], late, other_tracker[1:]):
        for gain, value in zip(gains, received.values()):
            piece = piece + gain * value.astype(jnp.float32)
        tracker_next = lax.dynamic_update_slice(tracker_next, piece.astype(jnp.bfloat16), (lo, 0))
    return (params_next[None], tracker_next[None])


def solution(mesh):
    placed = (P("grp", "blk", None), P("grp", "blk", None), P("grp", "blk"), P("grp", None))
    return jax.shard_map(
        step,
        mesh=mesh,
        in_specs=placed,
        out_specs=(P("grp", "blk", None), P("grp", "blk", None)),
        check_vma=False,
    )
```

profile of v0, /device:TPU:0, one launch (start us, length us, event | category | flops | bytes accessed | tf_op | source)
XLA Modules:
  0.0 167.3 jit_solution(6527862541646015390)
XLA Ops:
  0.6 0.0 copy-start
  0.6 1.5 slice_bitcast_fusion.3
  2.2 3.0 %collective-permute-start.4 = (bf16[8,4096]{1,0:T(8,128)(2,1)}, bf16[8,4096]{1,0:T(8,128)(2,1)}, u32[]{:S(2)}, u32[]{:S(2)}) collective-permute-start(bf16[8,4096]{1,0:T(8,128)(2,1)} %slice_bitcast_fusion.3), channel_id=1, source_target_pairs={{0,1},{2,3},{4,5},{6,7},{8,9},{10,11},{12,13},{14,15},{16,17},{18,... | collective-permute-start | bytes 196616 | tf_op jit(solution)/shard_map/ppermute | solution.py:49
  5.2 0.7 collective-permute-start.6
  5.9 0.0 copy-start.4
  5.9 2.4 %collective-permute-start = (bf16[448,4096]{1,0:T(8,128)(2,1)}, bf16[448,4096]{1,0:T(8,128)(2,1)}, u32[]{:S(2)}, u32[]{:S(2)}) collective-permute-start(bf16[448,4096]{1,0:T(8,128)(2,1)} %bitcast.51), channel_id=1, source_target_pairs={{0,16},{16,0},{1,17},{17,1},{2,18},{18,2},{3,19},{19,3},{4,20},{20... | collective-permute-start | bytes 11010056 | tf_op jit(solution)/shard_map/ppermute | solution.py:35
  8.3 3.5 %slice_bitcast_fusion = bf16[320,4096]{1,0:T(8,128)(2,1)} fusion(bf16[1,448,4096]{2,1,0:T(8,128)(2,1)} %param.5), kind=kLoop, calls=%fused_computation.9 | loop fusion | bytes 5242880 | tf_op jit(solution)/shard_map/slice | solution.py:208
  11.8 0.0 collective-permute-start.1
  11.8 2.1 %slice_bitcast_fusion.1 = bf16[96,4096]{1,0:T(8,128)(2,1)} fusion(bf16[1,448,4096]{2,1,0:T(8,128)(2,1)} %param.5), kind=kLoop, calls=%fused_computation.16 | loop fusion | bytes 1572864 | tf_op jit(solution)/shard_map/slice | solution.py:208
  13.9 2.0 %collective-permute-start.2 = (bf16[96,4096]{1,0:T(8,128)(2,1)}, bf16[96,4096]{1,0:T(8,128)(2,1)}, u32[]{:S(2)}, u32[]{:S(2)}) collective-permute-start(bf16[96,4096]{1,0:T(8,128)(2,1)} %slice_bitcast_fusion.1), channel_id=1, source_target_pairs={{0,16},{16,0},{1,17},{17,1},{2,18},{18,2},{3,19},{19,3},{4,20},{20... | collective-permute-start | bytes 2359304 | tf_op jit(solution)/shard_map/ppermute | solution.py:35
  15.9 0.9 slice_bitcast_fusion.2
  16.8 0.6 constant_dynamic-slice_fusion.target_ref
  17.5 0.1 copy.7
  17.6 4.1 %fusion.5.part_ref = f32[4,2,2,8,4096]{4,3,2,1,0:T(8,128)} fusion(bf16[4,2,2,8,448]{4,3,2,1,0:T(8,128)(2,1)S(1)} %bitcast.56, bf16[1,448,4096]{2,1,0:T(8,128)(2,1)} %param.4), kind=kOutput, calls=%fused_computation.7 | convolution fusion | flops 469762048 | bytes 5881856 | tf_op jit(solution)/shard_map/dot_general | solution.py:213
  21.7 35.5 %residual.3 = bf16[4,2,2,8,4096]{4,3,2,1,0:T(8,128)(2,1)} custom-call(f32[4,2,2,8,4096]{4,3,2,1,0:T(8,128)} %fusion.5.part_ref, bf16[8,4096]{1,0:T(8,128)(2,1)} %constant_dynamic-slice_fusion.target_ref), custom_call_target="tpu_custom_call" | custom-call | bytes 52428800 | tf_op jit(solution)/shard_map/residual/pallas_call | solution.py:149
  57.3 1.6 collective-permute-start.3
  58.9 29.4 %collective-permute-done = bf16[448,4096]{1,0:T(8,128)(2,1)} collective-permute-done((bf16[448,4096]{1,0:T(8,128)(2,1)}, bf16[448,4096]{1,0:T(8,128)(2,1)}, u32[]{:S(2)}, u32[]{:S(2)}) %collective-permute-start) | collective-permute-done | bytes 3670048 | tf_op jit(solution)/shard_map/ppermute | solution.py:35
  88.3 1.3 collective-permute-start.5
  89.6 6.8 %fusion.2 = bf16[448,4096]{1,0:T(8,128)(2,1)S(1)} fusion(bf16[1,448,4096]{2,1,0:T(8,128)(2,1)} %param.5, bf16[448,4096]{1,0:T(8,128)(2,1)} %collective-permute-done, f32[]{:T(128)} %add.62, f32[]{:T(128)S(6)} %add.58, bf16[1,448,4096]{2,1,0:T(8,128)(2,1)} %param.4), kind=kLoop, calls=%fused_computation.4 | loop fusion | flops 16515072 | bytes 14680072 | tf_op jit(solution)/shard_map/convert_element_type | solution.py:217
  96.4 0.0 copy-start.2
  96.4 2.1 %fusion.20 = f32[4096,128]{0,1:T(8,128)} fusion(bf16[448,4096]{1,0:T(8,128)(2,1)S(1)} %fusion.2, bf16[128,448]{0,1:T(8,128)(2,1)S(1)} %copy-done.4), kind=kOutput, calls=%fused_computation.30 | convolution fusion | flops 469762048 | bytes 5881856 | tf_op jit(solution)/shard_map/dot_general | solution.py:218
  98.5 0.4 copy-done.2
  98.9 39.3 %residual.2 = bf16[4,2,2,8,4096]{4,3,2,1,0:T(8,128)(2,1)} custom-call(f32[4,2,2,8,4096]{4,3,2,1,0:T(8,128)} %bitcast.52, bf16[8,4096]{1,0:T(8,128)(2,1)} %constant_dynamic-slice_fusion.target_ref), custom_call_target="tpu_custom_call" | custom-call | bytes 52428800 | tf_op jit(solution)/shard_map/residual/pallas_call | solution.py:149
  138.2 3.6 %fusion.4.base_ref = f32[448,4096]{1,0:T(8,128)S(1)} fusion(bf16[1,448,4096]{2,1,0:T(8,128)(2,1)} %param.5, f32[]{:T(128)S(6)} %add.58, bf16[128,4096]{1,0:T(8,128)(2,1)S(1)} %bitcast.53, bf16[128,4096]{1,0:T(8,128)(2,1)} %bitcast.54, bf16[128,448]{0,1:T(8,128)(2,1)S(1)} %neg.3, bf16[128,448]{0,1:T(8,128)(2,1)S(1)} %copy-done.4), kind=kOutput, calls=%fused_computation.6 | convolution fusion | flops 951517184 | bytes 13336580 | tf_op jit(solution)/shard_map/dot_general | solution.py:220
  141.8 2.9 %copy-done.1 = f32[448,4096]{1,0:T(8,128)} copy-done((f32[448,4096]{1,0:T(8,128)}, f32[448,4096]{1,0:T(8,128)S(1)}, u32[]{:S(2)}) %copy-start.1) | copy-done | bytes 7340056
  144.8 4.8 %add_others.1 = bf16[448,4096]{1,0:T(8,128)(2,1)} custom-call(f32[1]{0:T(128)} %bitcast.3.weights_ref, f32[448,4096]{1,0:T(8,128)} %copy-done.1, bf16[320,4096]{1,0:T(8,128)(2,1)} %collective-permute-done.1.refs_0_), custom_call_target="tpu_custom_call" | custom-call | flops 5242880 | bytes 10485760 | tf_op jit(solution)/shard_map/add_others/pallas_call | solution.py:181
  149.5 11.8 %collective-permute-done.2 = bf16[96,4096]{1,0:T(8,128)(2,1)} collective-permute-done((bf16[96,4096]{1,0:T(8,128)(2,1)}, bf16[96,4096]{1,0:T(8,128)(2,1)}, u32[]{:S(2)}, u32[]{:S(2)}) %collective-permute-start.2) | collective-permute-done | bytes 786464 | tf_op jit(solution)/shard_map/ppermute | solution.py:35
  161.3 2.2 %fusion.11 = bf16[1,448,4096]{2,1,0:T(8,128)(2,1)} fusion(bf16[1,448,4096]{2,1,0:T(8,128)(2,1)} %bitcast.55, f32[96,4096]{1,0:T(8,128)S(1)} %slice-done, bf16[96,4096]{1,0:T(8,128)(2,1)} %collective-permute-done.2, f32[]{:T(128)} %add.62), kind=kLoop, calls=%fused_computation.15 | loop fusion | flops 1572864 | bytes 3146240 | tf_op jit(solution)/shard_map/dynamic_update_slice | solution.py:235
  163.5 1.9 %collective-permute-done.3 = bf16[24,4096]{1,0:T(8,128)(2,1)S(1)} collective-permute-done((bf16[24,4096]{1,0:T(8,128)(2,1)S(1)}, bf16[24,4096]{1,0:T(8,128)(2,1)S(1)}, u32[]{:S(2)}, u32[]{:S(2)}) %collective-permute-start.3) | collective-permute-done | bytes 196640 | tf_op jit(solution)/shard_map/ppermute | solution.py:35
  165.4 0.7 fusion.16
  166.2 0.4 collective-permute-done.5
  166.6 0.7 fusion.18
  (15 shorter events, 0.1 us)
Async XLA Ops:
  0.6 16.2 %copy-start = (bf16[128,4096]{1,0:T(8,128)(2,1)S(1)}, bf16[128,4096]{1,0:T(8,128)(2,1)}, u32[]{:S(2)}) copy-start(bf16[128,4096]{1,0:T(8,128)(2,1)} %param.7) | copy-start | bytes 3145732
  2.2 55.1 %collective-permute-start.4 = (bf16[8,4096]{1,0:T(8,128)(2,1)}, bf16[8,4096]{1,0:T(8,128)(2,1)}, u32[]{:S(2)}, u32[]{:S(2)}) collective-permute-start(bf16[8,4096]{1,0:T(8,128)(2,1)} %slice_bitcast_fusion.3), channel_id=1, source_target_pairs={{0,1},{2,3},{4,5},{6,7},{8,9},{10,11},{12,13},{14,15},{16,17},{18,... | collective-permute-start | bytes 196616 | tf_op jit(solution)/shard_map/ppermute | solution.py:49
  5.2 161.0 %collective-permute-start.6 = (bf16[8,4096]{1,0:T(8,128)(2,1)}, bf16[8,4096]{1,0:T(8,128)(2,1)S(1)}, u32[]{:S(2)}, u32[]{:S(2)}) collective-permute-start(bf16[8,4096]{1,0:T(8,128)(2,1)} %slice_bitcast_fusion.3), channel_id=1, source_target_pairs={{1,17},{3,19},{5,21},{7,23},{9,25},{11,27},{13,29},{15,31},{17,1},... | collective-permute-start | bytes 196616 | tf_op jit(solution)/shard_map/ppermute | solution.py:51
  5.9 11.6 %copy-start.4 = (bf16[128,448]{0,1:T(8,128)(2,1)S(1)}, bf16[128,448]{0,1:T(8,128)(2,1)}, u32[]{:S(2)}) copy-start(bf16[128,448]{0,1:T(8,128)(2,1)} %param.6) | copy-start | bytes 344068
  5.9 82.4 %collective-permute-start = (bf16[448,4096]{1,0:T(8,128)(2,1)}, bf16[448,4096]{1,0:T(8,128)(2,1)}, u32[]{:S(2)}, u32[]{:S(2)}) collective-permute-start(bf16[448,4096]{1,0:T(8,128)(2,1)} %bitcast.51), channel_id=1, source_target_pairs={{0,16},{16,0},{1,17},{17,1},{2,18},{18,2},{3,19},{19,3},{4,20},{20... | collective-permute-start | bytes 11010056 | tf_op jit(solution)/shard_map/ppermute | solution.py:35
  11.8 133.0 %collective-permute-start.1 = (bf16[320,4096]{1,0:T(8,128)(2,1)}, bf16[320,4096]{1,0:T(8,128)(2,1)}, u32[]{:S(2)}, u32[]{:S(2)}) collective-permute-start(bf16[320,4096]{1,0:T(8,128)(2,1)} %slice_bitcast_fusion), channel_id=1, source_target_pairs={{0,16},{16,0},{1,17},{17,1},{2,18},{18,2},{3,19},{19,3},{4,20},{20... | collective-permute-start | bytes 7864328 | tf_op jit(solution)/shard_map/ppermute | solution.py:35
  13.9 147.4 %collective-permute-start.2 = (bf16[96,4096]{1,0:T(8,128)(2,1)}, bf16[96,4096]{1,0:T(8,128)(2,1)}, u32[]{:S(2)}, u32[]{:S(2)}) collective-permute-start(bf16[96,4096]{1,0:T(8,128)(2,1)} %slice_bitcast_fusion.1), channel_id=1, source_target_pairs={{0,16},{16,0},{1,17},{17,1},{2,18},{18,2},{3,19},{19,3},{4,20},{20... | collective-permute-start | bytes 2359304 | tf_op jit(solution)/shard_map/ppermute | solution.py:35
  57.3 108.2 %collective-permute-start.3 = (bf16[24,4096]{1,0:T(8,128)(2,1)S(1)}, bf16[24,4096]{1,0:T(8,128)(2,1)S(1)}, u32[]{:S(2)}, u32[]{:S(2)}) collective-permute-start(bf16[24,4096]{1,0:T(8,128)(2,1)S(1)} %slice_bitcast_fusion.2), channel_id=1, source_target_pairs={{0,16},{16,0},{1,17},{17,1},{2,18},{18,2},{3,19},{19,3},{4,20},{20... | collective-permute-start | bytes 589832 | tf_op jit(solution)/shard_map/ppermute | solution.py:35
  88.3 78.3 %collective-permute-start.5 = (bf16[8,4096]{1,0:T(8,128)(2,1)}, bf16[8,4096]{1,0:T(8,128)(2,1)S(1)}, u32[]{:S(2)}, u32[]{:S(2)}) collective-permute-start(bf16[8,4096]{1,0:T(8,128)(2,1)} %collective-permute-done.4), channel_id=1, source_target_pairs={{1,16},{3,18},{5,20},{7,22},{9,24},{11,26},{13,28},{15,30},{17,0},... | collective-permute-start | bytes 196616 | tf_op jit(solution)/shard_map/ppermute | solution.py:50
  96.4 2.5 %copy-start.2 = (bf16[448,4096]{1,0:T(8,128)(2,1)}, bf16[448,4096]{1,0:T(8,128)(2,1)S(1)}, u32[]{:S(2)}) copy-start(bf16[448,4096]{1,0:T(8,128)(2,1)S(1)} %fusion.2) | copy-start | bytes 11010052
  96.4 41.9 %copy-start.3 = (bf16[4,2,2,8,4096]{4,3,2,1,0:T(8,128)(2,1)S(1)}, bf16[4,2,2,8,4096]{4,3,2,1,0:T(8,128)(2,1)}, u32[]{:S(2)}) copy-start(bf16[4,2,2,8,4096]{4,3,2,1,0:T(8,128)(2,1)} %residual.3) | copy-start | bytes 3145732
  141.8 2.9 %copy-start.1 = (f32[448,4096]{1,0:T(8,128)}, f32[448,4096]{1,0:T(8,128)S(1)}, u32[]{:S(2)}) copy-start(f32[448,4096]{1,0:T(8,128)S(1)} %fusion.4.base_ref) | copy-start | bytes 22020100
  144.8 16.6 %slice-start = ((f32[448,4096]{1,0:T(8,128)}), f32[96,4096]{1,0:T(8,128)S(1)}, s32[]{:S(2)}) async-start(f32[448,4096]{1,0:T(8,128)} %copy-done.1), calls=%async_computation | async-start | bytes 3145728 | tf_op jit(solution)/shard_map/slice | solution.py:227
  144.8 20.7 %slice-start.1 = ((f32[448,4096]{1,0:T(8,128)}), f32[24,4096]{1,0:T(8,128)S(1)}, s32[]{:S(2)}) async-start(f32[448,4096]{1,0:T(8,128)} %copy-done.1), calls=%async_computation.1 | async-start | bytes 786432 | tf_op jit(solution)/shard_map/slice | solution.py:227
  149.5 17.1 %slice-start.2 = ((f32[448,4096]{1,0:T(8,128)}), f32[8,4096]{1,0:T(8,128)S(1)}, s32[]{:S(2)}) async-start(f32[448,4096]{1,0:T(8,128)} %copy-done.1), calls=%async_computation.2 | async-start | bytes 262144 | tf_op jit(solution)/shard_map/slice | solution.py:227
where the time goes:
time: 168 us; the launch traced here: 167 us
  Pallas kernels  79.6 us (47%)
  waiting for transfers between devices  43.5 us (26%)
  local copies, waits for them, and re-layouts  12.2 us (7%)
  starting transfers between devices  11 us (7%)
  other arithmetic  10.4 us (6%)
  matrix products  9.75 us (6%)
    pallas_call x2, Pallas kernels, residual(): pl.pallas_call(functools.partial(residual_kernel, z_size), out_shape=jax....  74.8 us
    ppermute x4, waiting for transfers between devices, exchange(): return {(-1, 1): lax.ppermute(value, 'grp', [(0, 1), (1, 0)])}  43.1 us
    slice x4, local copies, waits for them, and re-layouts, step(): slices = [tracker[lo:hi] for lo, hi in cuts]  8.11 us
    convert_element_type x1, other arithmetic, step(): params_next = (mixed(params, other_params, weights) - step_size * tracker...  6.77 us
    ppermute x4, starting transfers between devices, exchange(): return {(-1, 1): lax.ppermute(value, 'grp', [(0, 1), (1, 0)])}  6.04 us
    pallas_call x1, Pallas kernels, add_others(): pl.pallas_call(functools.partial(add_kernel, len(others)), grid=(count,),...  4.76 us
    dot_general x1, matrix products, step(): output_old = jnp.dot(hidden, params, preferred_element_type=jnp.float32)  4.07 us
    dynamic_update_slice x3, other arithmetic, step(): lax.dynamic_update_slice(tracker_next, piece.astype(jnp.bfloat16), (lo, 0))  3.59 us
  transfers between devices with their start and end apart: 7, of which 4 were waited for; matrix products, arithmetic and copies ran while one was open for 16% of the time, Pallas kernels for 48%

commit v1 on v0

--- a/solution.py
+++ b/solution.py
@@ -41,15 +41,8 @@
     return received
 
 
-def exchange_uneven(value, groups, n):
-    if groups != 2 or n % 2:
-        return exchange(value, groups)
-    both = ("grp", "blk")
-    sides = [(g, b) for g in range(groups) for b in range(0, n, 2)]
-    lent = lax.ppermute(value, both, [(g * n + b, g * n + b + 1) for g, b in sides])
-    for_even = lax.ppermute(lent, both, [(g * n + b + 1, (1 - g) * n + b) for g, b in sides])
-    for_odd = lax.ppermute(value, both, [(g * n + b + 1, (1 - g) * n + b + 1) for g, b in sides])
-    return {(-1, 1): for_even + for_odd}
+def helpers(z_size):
+    return [3] + [4 * z + 1 for z in range(1, z_size)]
 
 
 def mixed(own, others, weights):
@@ -62,10 +55,13 @@
 PIECES = 4
 
 
-def residual_kernel(
-    z_size, part_ref, target_ref, out_ref, core_in, core_sum, y_in, y_sum, z_in, *sems
-):
-    (core_s, core_r, y_s, y_r, z_s, z_r, gz_s, gz_r, gy_s, gy_r, gc_s, gc_r) = sems
+def residual_kernel(z_size, lends, part_ref, target_ref, *refs):
+    if lends is not None:
+        near_ref, out_ref, far_ref, *refs = refs
+    else:
+        out_ref, *refs = refs
+    core_in, core_sum, y_in, y_sum, z_in, *sems = refs
+    (core_s, core_r, y_s, y_r, z_s, z_r, gz_s, gz_r, gy_s, gy_r, gc_s, gc_r) = sems[:12]
     me = lax.axis_index("blk")
     c = lax.rem(me, 2)
     y = lax.rem(lax.div(me, 2), 2)
@@ -77,10 +73,43 @@
     width = target_ref.shape[-1] // PIECES
     columns = [pl.ds(q * width, width) for q in range(PIECES)]
 
+    greeted = [core_peer, y_peer, *z_peers]
+    if lends is not None:
+        relay_s, relay_r = sems[12:]
+        greeted += [z * 4 + (1 - y) * 2 + 1 - c, *[spot * 4 + y * 2 + 1 - c for spot in z_spots]]
+        home = (lax.axis_index("grp") == (1 if lends else 0)) & (me == 0)
+        helps = [
+            (lax.axis_index("grp") == (1 if lends else 0)) & (me == spot) for spot in helpers(z_size)
+        ]
+        receives = functools.reduce(lambda a, b: a | b, helps) if lends else home
+
+        @pl.when(jnp.logical_not(receives))
+        def _():
+            far_ref[...] = jnp.zeros_like(far_ref)
+
     barrier = pltpu.get_barrier_semaphore()
-    for peer in [core_peer, y_peer, *z_peers]:
+    for peer in greeted:
         pl.semaphore_signal(barrier, inc=1, device_id={"blk": peer}, device_id_type=MESH)
-    pl.semaphore_wait(barrier, z_size + 1)
+    pl.semaphore_wait(barrier, len(greeted))
+
+    def relay(j):
+        length = target_ref.shape[-1] // z_size
+        at = pl.ds(j * length, length)
+        return pltpu.make_async_remote_copy(
+            src_ref=near_ref.at[:, at] if lends else near_ref,
+            dst_ref=far_ref if lends else far_ref.at[:, at],
+            send_sem=relay_s.at[j],
+            recv_sem=relay_r.at[j],
+            device_id={"blk": helpers(z_size)[j] if lends else 0},
+            device_id_type=MESH,
+        )
+
+    def relay_all(act):
+        for j in range(z_size):
+            pl.when(home if lends else helps[j])(functools.partial(act, j))
+
+    if lends is not None:
+        relay_all(lambda j: relay(j).start())
 
     def send(src, dst, send_sem, recv_sem, peer):
         copy = pltpu.make_async_remote_copy(
@@ -137,20 +166,31 @@
         give_core.append(send(mine, mine, gc_s.at[q], gc_r.at[q], core_peer))
     for copy in give_core:
         copy.wait_recv()
+    if lends is not None:
+        for j in range(z_size):
+            pl.when(helps[j] if lends else home)(lambda j=j: relay(j).wait_recv())
+        relay_all(lambda j: relay(j).wait_send())
     for copy in [*over_core, *over_y, *sum(over_z, []), *sum(give_z, []), *give_y, *give_core]:
         copy.wait_send()
 
 
-def residual(output, own_target, n, which):
+def residual(output, own_target, n, which, lends=None, near=None):
     tokens, width = output.shape
     share, z_size = tokens // n, n // 4
     one = pltpu.SemaphoreType.DMA((PIECES,))
     many = pltpu.SemaphoreType.DMA((PIECES, z_size - 1))
-    resid = pl.pallas_call(
-        functools.partial(residual_kernel, z_size),
-        out_shape=jax.ShapeDtypeStruct((z_size, 2, 2, share, width), jnp.bfloat16),
-        in_specs=[pl.BlockSpec(memory_space=pltpu.VMEM)] * 2,
-        out_specs=pl.BlockSpec(memory_space=pltpu.VMEM),
+    there = pl.BlockSpec(memory_space=pltpu.VMEM)
+    shapes = [jax.ShapeDtypeStruct((z_size, 2, 2, share, width), jnp.bfloat16)]
+    operands = [output.reshape(z_size, 2, 2, share, width), own_target]
+    if lends is not None:
+        operands.append(near)
+        wide = width // z_size if lends else width
+        shapes.append(jax.ShapeDtypeStruct((near.shape[0], wide), near.dtype))
+    resid, *far = pl.pallas_call(
+        functools.partial(residual_kernel, z_size, lends),
+        out_shape=shapes,
+        in_specs=[there] * len(operands),
+        out_specs=[there] * len(shapes),
         scratch_shapes=[
             pltpu.VMEM((z_size, 2, share, width), jnp.float32),
             pltpu.VMEM((z_size, 2, share, width), jnp.float32),
@@ -158,12 +198,13 @@
             pltpu.VMEM((z_size, share, width), jnp.float32),
             pltpu.VMEM((z_size - 1, share, width), jnp.float32),
             one, one, one, one, many, many, many, many, one, one, one, one,
+            *([] if lends is None else [pltpu.SemaphoreType.DMA((z_size,))] * 2),
         ],
         compiler_params=pltpu.CompilerParams(collective_id=which, has_side_effects=True),
         cost_estimate=pl.CostEstimate(flops=0, bytes_accessed=100 * tokens * width, transcendentals=0),
         name="residual",
-    )(output.reshape(z_size, 2, 2, share, width), own_target)
-    return resid.reshape(tokens, width)
+    )(*operands)
+    return (resid.reshape(tokens, width), *far)
 
 
 def add_kernel(count, weights_ref, base_ref, *refs):
@@ -202,21 +243,36 @@
     rows = params.shape[0]
     block = 16
     first = rows * 5 // 7 // 16 * 16
-    ends = sorted({first, max(first, rows - 32), max(first, rows - 8), rows})
+    ends = sorted({first, max(first, rows - 40), max(first, rows - 16), rows})
     cuts = list(zip([0, *ends[:-1]], ends))
     other_params = exchange(params, groups)
     slices = [tracker[lo:hi] for lo, hi in cuts]
+    output_old = jnp.dot(hidden, params, preferred_element_type=jnp.float32)
+    relayed = groups == 2 and n >= 8
+    if relayed:
+        resid_old, lent = residual(output_old, own_target, n, 0, True, slices[-1])
+        both, spots = ("grp", "blk"), helpers(n // 4)
+        carried = lax.ppermute(lent, both, [(n + spot, spot) for spot in spots])
+    else:
+        (resid_old,) = residual(output_old, own_target, n, 0)
     other_tracker = []
     for piece in slices[:-1]:
         other_tracker.append(exchange(piece, groups))
-    other_tracker.append(exchange_uneven(slices[-1], groups, n))
-    output_old = jnp.dot(hidden, params, preferred_element_type=jnp.float32)
-    resid_old = residual(output_old, own_target, n, 0)
     params_next = (
         mixed(params, other_params, weights) - step_size * tracker.astype(jnp.float32)
     ).astype(jnp.bfloat16)
     output_new = jnp.dot(hidden, params_next, preferred_element_type=jnp.float32)
-    resid_new = residual(output_new, own_target, n, 1)
+    if relayed:
+        pairs = [(b, n + b) for b in range(n)] + [(n + b, b) for b in range(1, n)]
+        last = {(-1, 1): lax.ppermute(slices[-1], both, pairs)}
+    else:
+        last = exchange(slices[-1], groups)
+    if relayed:
+        resid_new, returned = residual(output_new, own_target, n, 1, False, carried)
+        last = {key: value + returned for key, value in last.items()}
+    else:
+        (resid_new,) = residual(output_new, own_target, n, 1)
+    other_tracker.append(last)
     change = lax.dot_general(
         jnp.concatenate([hidden, -hidden], 0),
         jnp.concatenate([resid_new, resid_old], 0),

time: 168 us -> 163 us (0.970)
  waiting for transfers between devices: 43.5 us -> 40.3 us
    ppermute x4, waiting for transfers between devices: 43.1 us -> 40.3 us  [exchange(): return {(-1, 1): lax.ppermute(value, 'grp', [(0, 1), (1, 0)])}]
    ppermute x3 -> x2, starting transfers between devices: 4.94 us -> 2.8 us  [the longest x1 2 us: step(): last = {(-1, 1): lax.ppermute(slices[-1], both, pairs)}]
    unnamed x11 -> x17, local copies, waits for them, and re-layouts: 3.47 us -> 4.99 us
  transfers between devices with their start and end apart: 7 -> 6, of which waited for: 4 -> 4; matrix products, arithmetic and copies ran while one was open for 16% -> 17% of each run, Pallas kernels for 48% -> 48%
where the time goes in v1:
time: 163 us
  Pallas kernels  78.5 us (48%)
  waiting for transfers between devices  40.3 us (25%)
  local copies, waits for them, and re-layouts  13 us (8%)
  other arithmetic  10.4 us (6%)
  starting transfers between devices  9.87 us (6%)
  matrix products  9.73 us (6%)
    pallas_call x2, Pallas kernels, residual(): pl.pallas_call(functools.partial(residual_kernel, z_size, lends), out_sha...  73.7 us
    ppermute x4, waiting for transfers between devices, exchange(): return {(-1, 1): lax.ppermute(value, 'grp', [(0, 1), (1, 0)])}  40.3 us
    slice x4, local copies, waits for them, and re-layouts, step(): slices = [tracker[lo:hi] for lo, hi in cuts]  7.43 us
    ppermute x4, starting transfers between devices, exchange(): return {(-1, 1): lax.ppermute(value, 'grp', [(0, 1), (1, 0)])}  7.07 us
    convert_element_type x1, other arithmetic, step(): params_next = (mixed(params, other_params, weights) - step_size * tracker...  6.77 us
    unnamed x17, local copies, waits for them, and re-layouts  4.99 us
    pallas_call x1, Pallas kernels, add_others(): pl.pallas_call(functools.partial(add_kernel, len(others)), grid=(count,),...  4.74 us
    dot_general x1, matrix products, step(): output_old = jnp.dot(hidden, params, preferred_element_type=jnp.float32)  4.07 us
  transfers between devices with their start and end apart: 6, of which 4 were waited for; matrix products, arithmetic and copies ran while one was open for 17% of the time, Pallas kernels for 48%

profile of v1, /device:TPU:0, one launch (start us, length us, event | category | flops | bytes accessed | tf_op | source)
XLA Modules:
  0.0 162.6 jit_solution(13166979778585951578)
XLA Ops:
  0.6 0.0 copy-start
  0.6 3.0 %collective-permute-start = (bf16[448,4096]{1,0:T(8,128)(2,1)}, bf16[448,4096]{1,0:T(8,128)(2,1)}, u32[]{:S(2)}, u32[]{:S(2)}) collective-permute-start(bf16[448,4096]{1,0:T(8,128)(2,1)} %bitcast.51), channel_id=1, source_target_pairs={{0,16},{16,0},{1,17},{17,1},{2,18},{18,2},{3,19},{19,3},{4,20},{20... | collective-permute-start | bytes 11010056 | tf_op jit(solution)/shard_map/ppermute | solution.py:35
  3.7 0.9 slice_bitcast_fusion.3.refs_0_
  4.6 0.0 copy-start.5
  4.6 2.0 %collective-permute-start.5 = (bf16[16,4096]{1,0:T(8,128)(2,1)S(1)}, bf16[16,4096]{1,0:T(8,128)(2,1)S(1)}, u32[]{:S(2)}, u32[]{:S(2)}) collective-permute-start(bf16[16,4096]{1,0:T(8,128)(2,1)S(1)} %slice_bitcast_fusion.3.refs_0_), channel_id=1, source_target_pairs={{0,16},{1,17},{2,18},{3,19},{4,20},{5,21},{6,22},{7,23},{8,24},{9,... | collective-permute-start | bytes 393224 | tf_op jit(solution)/shard_map/ppermute | solution.py:267
  6.6 1.0 copy.7
  7.6 4.1 %fusion.5.part_ref = f32[4,2,2,8,4096]{4,3,2,1,0:T(8,128)} fusion(bf16[4,2,2,8,448]{4,3,2,1,0:T(8,128)(2,1)S(1)} %bitcast.56, bf16[1,448,4096]{2,1,0:T(8,128)(2,1)} %param.4), kind=kOutput, calls=%fused_computation.7 | convolution fusion | flops 469762048 | bytes 5881856 | tf_op jit(solution)/shard_map/dot_general | solution.py:250
  11.7 0.6 constant_dynamic-slice_fusion.target_ref
  12.3 37.1 %residual.2 = (bf16[4,2,2,8,4096]{4,3,2,1,0:T(8,128)(2,1)}, bf16[16,1024]{1,0:T(8,128)(2,1)}) custom-call(f32[4,2,2,8,4096]{4,3,2,1,0:T(8,128)} %fusion.5.part_ref, bf16[8,4096]{1,0:T(8,128)(2,1)} %constant_dynamic-slice_fusion.target_ref, bf16[16,4096]{1,0:T(8,128)(2,1)} %copy-done.5), custom_call_target="tpu_custom_call" | custom-call | bytes 52428800 | tf_op jit(solution)/shard_map/residual/pallas_call | solution.py:189
  49.5 0.0 copy-start.3
  49.5 0.8 collective-permute-start.1
  50.3 3.5 %slice_bitcast_fusion = bf16[320,4096]{1,0:T(8,128)(2,1)} fusion(bf16[1,448,4096]{2,1,0:T(8,128)(2,1)} %param.5), kind=kLoop, calls=%fused_computation.9 | loop fusion | bytes 5242880 | tf_op jit(solution)/shard_map/slice | solution.py:249
  53.8 1.5 collective-permute-start.2
  55.3 2.0 %slice_bitcast_fusion.1 = bf16[88,4096]{1,0:T(8,128)(2,1)} fusion(bf16[1,448,4096]{2,1,0:T(8,128)(2,1)} %param.5), kind=kLoop, calls=%fused_computation.16 | loop fusion | bytes 1441792 | tf_op jit(solution)/shard_map/slice | solution.py:249
  57.3 0.6 collective-permute-start.3
  57.9 0.9 slice_bitcast_fusion.2
  58.9 25.3 %collective-permute-done = bf16[448,4096]{1,0:T(8,128)(2,1)} collective-permute-done((bf16[448,4096]{1,0:T(8,128)(2,1)}, bf16[448,4096]{1,0:T(8,128)(2,1)}, u32[]{:S(2)}, u32[]{:S(2)}) %collective-permute-start) | collective-permute-done | bytes 3670048 | tf_op jit(solution)/shard_map/ppermute | solution.py:35
  84.2 2.0 %collective-permute-start.4 = (bf16[24,4096]{1,0:T(8,128)(2,1)S(1)}, bf16[24,4096]{1,0:T(8,128)(2,1)S(1)}, u32[]{:S(2)}, u32[]{:S(2)}) collective-permute-start(bf16[24,4096]{1,0:T(8,128)(2,1)S(1)} %slice_bitcast_fusion.2), channel_id=1, source_target_pairs={{0,16},{16,0},{1,17},{17,1},{2,18},{18,2},{3,19},{19,3},{4,20},{20... | collective-permute-start | bytes 589832 | tf_op jit(solution)/shard_map/ppermute | solution.py:35
  86.2 6.8 %fusion.2 = bf16[448,4096]{1,0:T(8,128)(2,1)S(1)} fusion(bf16[1,448,4096]{2,1,0:T(8,128)(2,1)} %param.5, bf16[448,4096]{1,0:T(8,128)(2,1)} %collective-permute-done, f32[]{:T(128)} %add.62, f32[]{:T(128)S(6)} %add.58, bf16[1,448,4096]{2,1,0:T(8,128)(2,1)} %param.4), kind=kLoop, calls=%fused_computation.4 | loop fusion | flops 16515072 | bytes 14680072 | tf_op jit(solution)/shard_map/convert_element_type | solution.py:263
  93.0 2.1 %fusion.20 = f32[4096,128]{0,1:T(8,128)} fusion(bf16[448,4096]{1,0:T(8,128)(2,1)S(1)} %fusion.2, bf16[128,448]{0,1:T(8,128)(2,1)S(1)} %copy-done.3), kind=kOutput, calls=%fused_computation.30 | convolution fusion | flops 469762048 | bytes 5881856 | tf_op jit(solution)/shard_map/dot_general | solution.py:264
  95.1 0.4 copy-done.2
  95.5 0.6 copy-done.7
  96.1 36.6 %residual.3 = (bf16[4,2,2,8,4096]{4,3,2,1,0:T(8,128)(2,1)}, bf16[16,4096]{1,0:T(8,128)(2,1)}) custom-call(f32[4,2,2,8,4096]{4,3,2,1,0:T(8,128)} %bitcast.52, bf16[8,4096]{1,0:T(8,128)(2,1)} %constant_dynamic-slice_fusion.target_ref, bf16[16,1024]{1,0:T(8,128)(2,1)} %copy-done.7), custom_call_target="tpu_custom_call" | custom-call | bytes 52428800 | tf_op jit(solution)/shard_map/residual/pallas_call | solution.py:189
  132.7 3.6 %fusion.4.base_ref = f32[448,4096]{1,0:T(8,128)S(1)} fusion(bf16[1,448,4096]{2,1,0:T(8,128)(2,1)} %param.5, f32[]{:T(128)S(6)} %add.58, bf16[128,4096]{1,0:T(8,128)(2,1)S(1)} %bitcast.54, bf16[128,4096]{1,0:T(8,128)(2,1)} %bitcast.55, bf16[128,448]{0,1:T(8,128)(2,1)S(1)} %neg.3, bf16[128,448]{0,1:T(8,128)(2,1)S(1)} %copy-done.3), kind=kOutput, calls=%fused_computation.6 | convolution fusion | flops 951517184 | bytes 13336580 | tf_op jit(solution)/shard_map/dot_general | solution.py:276
  136.3 2.9 %copy-done.1 = f32[448,4096]{1,0:T(8,128)} copy-done((f32[448,4096]{1,0:T(8,128)}, f32[448,4096]{1,0:T(8,128)S(1)}, u32[]{:S(2)}) %copy-start.1) | copy-done | bytes 7340056
  139.3 3.4 %collective-permute-done.2.refs_0_ = bf16[320,4096]{1,0:T(8,128)(2,1)} collective-permute-done((bf16[320,4096]{1,0:T(8,128)(2,1)}, bf16[320,4096]{1,0:T(8,128)(2,1)}, u32[]{:S(2)}, u32[]{:S(2)}) %collective-permute-start.2) | collective-permute-done | bytes 2621472 | tf_op jit(solution)/shard_map/ppermute | solution.py:35
  142.7 4.7 %add_others.1 = bf16[448,4096]{1,0:T(8,128)(2,1)} custom-call(f32[1]{0:T(128)} %bitcast.3.weights_ref, f32[448,4096]{1,0:T(8,128)} %copy-done.1, bf16[320,4096]{1,0:T(8,128)(2,1)} %collective-permute-done.2.refs_0_), custom_call_target="tpu_custom_call" | custom-call | flops 5242880 | bytes 10485760 | tf_op jit(solution)/shard_map/add_others/pallas_call | solution.py:222
  147.5 10.7 %collective-permute-done.3 = bf16[88,4096]{1,0:T(8,128)(2,1)} collective-permute-done((bf16[88,4096]{1,0:T(8,128)(2,1)}, bf16[88,4096]{1,0:T(8,128)(2,1)}, u32[]{:S(2)}, u32[]{:S(2)}) %collective-permute-start.3) | collective-permute-done | bytes 720928 | tf_op jit(solution)/shard_map/ppermute | solution.py:35
  158.2 2.1 %fusion.11 = bf16[1,448,4096]{2,1,0:T(8,128)(2,1)} fusion(bf16[1,448,4096]{2,1,0:T(8,128)(2,1)} %bitcast.53, f32[88,4096]{1,0:T(8,128)S(1)} %slice-done, bf16[88,4096]{1,0:T(8,128)(2,1)} %collective-permute-done.3, f32[]{:T(128)} %add.62), kind=kLoop, calls=%fused_computation.15 | loop fusion | flops 1441792 | bytes 2884096 | tf_op jit(solution)/shard_map/dynamic_update_slice | solution.py:291
  160.3 0.8 collective-permute-done.4
  161.1 0.7 fusion.16
  161.9 0.7 fusion.18
  (19 shorter events, 0.1 us)
Async XLA Ops:
  0.6 11.1 %copy-start = (bf16[128,4096]{1,0:T(8,128)(2,1)S(1)}, bf16[128,4096]{1,0:T(8,128)(2,1)}, u32[]{:S(2)}) copy-start(bf16[128,4096]{1,0:T(8,128)(2,1)} %param.7) | copy-start | bytes 3145732
  0.6 83.5 %collective-permute-start = (bf16[448,4096]{1,0:T(8,128)(2,1)}, bf16[448,4096]{1,0:T(8,128)(2,1)}, u32[]{:S(2)}, u32[]{:S(2)}) collective-permute-start(bf16[448,4096]{1,0:T(8,128)(2,1)} %bitcast.51), channel_id=1, source_target_pairs={{0,16},{16,0},{1,17},{17,1},{2,18},{18,2},{3,19},{19,3},{4,20},{20... | collective-permute-start | bytes 11010056 | tf_op jit(solution)/shard_map/ppermute | solution.py:35
  4.6 7.7 %copy-start.5 = (bf16[16,4096]{1,0:T(8,128)(2,1)}, bf16[16,4096]{1,0:T(8,128)(2,1)S(1)}, u32[]{:S(2)}) copy-start(bf16[16,4096]{1,0:T(8,128)(2,1)S(1)} %slice_bitcast_fusion.3.refs_0_) | copy-start | bytes 393220
  4.6 157.3 %collective-permute-start.5 = (bf16[16,4096]{1,0:T(8,128)(2,1)S(1)}, bf16[16,4096]{1,0:T(8,128)(2,1)S(1)}, u32[]{:S(2)}, u32[]{:S(2)}) collective-permute-start(bf16[16,4096]{1,0:T(8,128)(2,1)S(1)} %slice_bitcast_fusion.3.refs_0_), channel_id=1, source_target_pairs={{0,16},{1,17},{2,18},{3,19},{4,20},{5,21},{6,22},{7,23},{8,24},{9,... | collective-permute-start | bytes 393224 | tf_op jit(solution)/shard_map/ppermute | solution.py:267
  49.5 8.4 %copy-start.3 = (bf16[128,448]{0,1:T(8,128)(2,1)S(1)}, bf16[128,448]{0,1:T(8,128)(2,1)}, u32[]{:S(2)}) copy-start(bf16[128,448]{0,1:T(8,128)(2,1)} %param.6) | copy-start | bytes 344068
  49.5 46.0 %collective-permute-start.1 = (bf16[16,1024]{1,0:T(8,128)(2,1)}, bf16[16,1024]{1,0:T(8,128)(2,1)S(1)}, u32[]{:S(2)}, u32[]{:S(2)}) collective-permute-start(bf16[16,1024]{1,0:T(8,128)(2,1)} %get-tuple-element.9), channel_id=1, source_target_pairs={{19,3},{21,5},{25,9},{29,13}} | collective-permute-start | bytes 98312 | tf_op jit(solution)/shard_map/ppermute | solution.py:255
  53.8 88.9 %collective-permute-start.2 = (bf16[320,4096]{1,0:T(8,128)(2,1)}, bf16[320,4096]{1,0:T(8,128)(2,1)}, u32[]{:S(2)}, u32[]{:S(2)}) collective-permute-start(bf16[320,4096]{1,0:T(8,128)(2,1)} %slice_bitcast_fusion), channel_id=1, source_target_pairs={{0,16},{16,0},{1,17},{17,1},{2,18},{18,2},{3,19},{19,3},{4,20},{20... | collective-permute-start | bytes 7864328 | tf_op jit(solution)/shard_map/ppermute | solution.py:35
  57.3 100.8 %collective-permute-start.3 = (bf16[88,4096]{1,0:T(8,128)(2,1)}, bf16[88,4096]{1,0:T(8,128)(2,1)}, u32[]{:S(2)}, u32[]{:S(2)}) collective-permute-start(bf16[88,4096]{1,0:T(8,128)(2,1)} %slice_bitcast_fusion.1), channel_id=1, source_target_pairs={{0,16},{16,0},{1,17},{17,1},{2,18},{18,2},{3,19},{19,3},{4,20},{20... | collective-permute-start | bytes 2162696 | tf_op jit(solution)/shard_map/ppermute | solution.py:35
  84.2 76.9 %collective-permute-start.4 = (bf16[24,4096]{1,0:T(8,128)(2,1)S(1)}, bf16[24,4096]{1,0:T(8,128)(2,1)S(1)}, u32[]{:S(2)}, u32[]{:S(2)}) collective-permute-start(bf16[24,4096]{1,0:T(8,128)(2,1)S(1)} %slice_bitcast_fusion.2), channel_id=1, source_target_pairs={{0,16},{16,0},{1,17},{17,1},{2,18},{18,2},{3,19},{19,3},{4,20},{20... | collective-permute-start | bytes 589832 | tf_op jit(solution)/shard_map/ppermute | solution.py:35
  93.0 2.5 %copy-start.2 = (bf16[448,4096]{1,0:T(8,128)(2,1)}, bf16[448,4096]{1,0:T(8,128)(2,1)S(1)}, u32[]{:S(2)}) copy-start(bf16[448,4096]{1,0:T(8,128)(2,1)S(1)} %fusion.2) | copy-start | bytes 11010052
  93.0 39.7 %copy-start.4 = (bf16[4,2,2,8,4096]{4,3,2,1,0:T(8,128)(2,1)S(1)}, bf16[4,2,2,8,4096]{4,3,2,1,0:T(8,128)(2,1)}, u32[]{:S(2)}) copy-start(bf16[4,2,2,8,4096]{4,3,2,1,0:T(8,128)(2,1)} %get-tuple-element.11) | copy-start | bytes 3145732
  95.5 0.6 copy-start.7
  136.3 3.0 %copy-start.1 = (f32[448,4096]{1,0:T(8,128)}, f32[448,4096]{1,0:T(8,128)S(1)}, u32[]{:S(2)}) copy-start(f32[448,4096]{1,0:T(8,128)S(1)} %fusion.4.base_ref) | copy-start | bytes 22020100
  142.7 15.5 %slice-start = ((f32[448,4096]{1,0:T(8,128)}), f32[88,4096]{1,0:T(8,128)S(1)}, s32[]{:S(2)}) async-start(f32[448,4096]{1,0:T(8,128)} %copy-done.1), calls=%async_computation | async-start | bytes 2883584 | tf_op jit(solution)/shard_map/slice | solution.py:283
  142.7 18.4 %slice-start.1 = ((f32[448,4096]{1,0:T(8,128)}), f32[24,4096]{1,0:T(8,128)S(1)}, s32[]{:S(2)}) async-start(f32[448,4096]{1,0:T(8,128)} %copy-done.1), calls=%async_computation.1 | async-start | bytes 786432 | tf_op jit(solution)/shard_map/slice | solution.py:283
  147.4 14.4 %slice-start.2 = ((f32[448,4096]{1,0:T(8,128)}), f32[16,4096]{1,0:T(8,128)S(1)}, s32[]{:S(2)}) async-start(f32[448,4096]{1,0:T(8,128)} %copy-done.1), calls=%async_computation.2 | async-start | bytes 524288 | tf_op jit(solution)/shard_map/slice | solution.py:283
  147.5 14.4 %copy-start.6 = (bf16[16,4096]{1,0:T(8,128)(2,1)S(1)}, bf16[16,4096]{1,0:T(8,128)(2,1)}, u32[]{:S(2)}) copy-start(bf16[16,4096]{1,0:T(8,128)(2,1)} %get-tuple-element.15) | copy-start | bytes 393220

commit v2 on v1

--- a/solution.py
+++ b/solution.py
@@ -42,7 +42,7 @@
 
 
 def helpers(z_size):
-    return [3] + [4 * z + 1 for z in range(1, z_size)]
+    return [2 * chip + 1 for chip in range(2 * z_size)]
 
 
 def mixed(own, others, weights):
@@ -57,7 +57,9 @@
 
 def residual_kernel(z_size, lends, part_ref, target_ref, *refs):
     if lends is not None:
-        near_ref, out_ref, far_ref, *refs = refs
+        near_ref, *refs = refs
+        home_ref, *refs = refs if not lends else [None, *refs]
+        out_ref, far_ref, *refs = refs
     else:
         out_ref, *refs = refs
     core_in, core_sum, y_in, y_sum, z_in, *sems = refs
@@ -76,16 +78,25 @@
     greeted = [core_peer, y_peer, *z_peers]
     if lends is not None:
         relay_s, relay_r = sems[12:]
-        greeted += [z * 4 + (1 - y) * 2 + 1 - c, *[spot * 4 + y * 2 + 1 - c for spot in z_spots]]
-        home = (lax.axis_index("grp") == (1 if lends else 0)) & (me == 0)
-        helps = [
-            (lax.axis_index("grp") == (1 if lends else 0)) & (me == spot) for spot in helpers(z_size)
-        ]
-        receives = functools.reduce(lambda a, b: a | b, helps) if lends else home
-
-        @pl.when(jnp.logical_not(receives))
-        def _():
-            far_ref[...] = jnp.zeros_like(far_ref)
+        greeted += [spot * 4 + y * 2 + 1 - c for spot in z_spots]
+        greeted += [spot * 4 + (1 - y) * 2 + 1 - c for spot in [z, *z_spots]]
+        length = target_ref.shape[-1] // (2 * z_size)
+        late_side = lax.axis_index("grp") == (1 if lends else 0)
+        travels = [late_side | (j >= z_size) for j in range(2 * z_size)]
+        homes = [(me == 0) & travel for travel in travels]
+        helps = [(me == spot) & travel for spot, travel in zip(helpers(z_size), travels)]
+        if lends:
+            fills = [(functools.reduce(lambda a, b: a | b, helps), pl.ds(0, length))]
+        else:
+            fills = [(home, pl.ds(j * length, length)) for j, home in enumerate(homes)]
+        for filled, at in fills:
+
+            @pl.when(jnp.logical_not(filled))
+            def _(at=at):
+                if lends or at.start >= home_ref.shape[-1]:
+                    far_ref[:, at] = jnp.zeros((far_ref.shape[0], length), far_ref.dtype)
+                else:
+                    far_ref[:, at] = home_ref[:, at]
 
     barrier = pltpu.get_barrier_semaphore()
     for peer in greeted:
@@ -93,7 +104,6 @@
     pl.semaphore_wait(barrier, len(greeted))
 
     def relay(j):
-        length = target_ref.shape[-1] // z_size
         at = pl.ds(j * length, length)
         return pltpu.make_async_remote_copy(
             src_ref=near_ref.at[:, at] if lends else near_ref,
@@ -105,8 +115,8 @@
         )
 
     def relay_all(act):
-        for j in range(z_size):
-            pl.when(home if lends else helps[j])(functools.partial(act, j))
+        for j in range(2 * z_size):
+            pl.when(homes[j] if lends else helps[j])(functools.partial(act, j))
 
     if lends is not None:
         relay_all(lambda j: relay(j).start())
@@ -167,14 +177,14 @@
     for copy in give_core:
         copy.wait_recv()
     if lends is not None:
-        for j in range(z_size):
-            pl.when(helps[j] if lends else home)(lambda j=j: relay(j).wait_recv())
+        for j in range(2 * z_size):
+            pl.when(helps[j] if lends else homes[j])(lambda j=j: relay(j).wait_recv())
         relay_all(lambda j: relay(j).wait_send())
     for copy in [*over_core, *over_y, *sum(over_z, []), *sum(give_z, []), *give_y, *give_core]:
         copy.wait_send()
 
 
-def residual(output, own_target, n, which, lends=None, near=None):
+def residual(output, own_target, n, which, lends=None, *near):
     tokens, width = output.shape
     share, z_size = tokens // n, n // 4
     one = pltpu.SemaphoreType.DMA((PIECES,))
@@ -183,9 +193,9 @@
     shapes = [jax.ShapeDtypeStruct((z_size, 2, 2, share, width), jnp.bfloat16)]
     operands = [output.reshape(z_size, 2, 2, share, width), own_target]
     if lends is not None:
-        operands.append(near)
-        wide = width // z_size if lends else width
-        shapes.append(jax.ShapeDtypeStruct((near.shape[0], wide), near.dtype))
+        operands += near
+        wide = width // (2 * z_size) if lends else width
+        shapes.append(jax.ShapeDtypeStruct((near[0].shape[0], wide), near[0].dtype))
     resid, *far = pl.pallas_call(
         functools.partial(residual_kernel, z_size, lends),
         out_shape=shapes,
@@ -198,7 +208,7 @@
             pltpu.VMEM((z_size, share, width), jnp.float32),
             pltpu.VMEM((z_size - 1, share, width), jnp.float32),
             one, one, one, one, many, many, many, many, one, one, one, one,
-            *([] if lends is None else [pltpu.SemaphoreType.DMA((z_size,))] * 2),
+            *([] if lends is None else [pltpu.SemaphoreType.DMA((2 * z_size,))] * 2),
         ],
         compiler_params=pltpu.CompilerParams(collective_id=which, has_side_effects=True),
         cost_estimate=pl.CostEstimate(flops=0, bytes_accessed=100 * tokens * width, transcendentals=0),
@@ -252,7 +262,12 @@
     if relayed:
         resid_old, lent = residual(output_old, own_target, n, 0, True, slices[-1])
         both, spots = ("grp", "blk"), helpers(n // 4)
-        carried = lax.ppermute(lent, both, [(n + spot, spot) for spot in spots])
+        inward = [(n + spot, spot) for spot in spots]
+        outward = [(spot, n + spot) for spot in spots[len(spots) // 2 :]]
+        width = params.shape[1]
+        beside = lax.ppermute(slices[-1][:, : width // 2], both, [(0, 1)])
+        home = lax.ppermute(beside, both, [(1, n)])
+        carried = lax.ppermute(lent, both, outward + inward)
     else:
         (resid_old,) = residual(output_old, own_target, n, 0)
     other_tracker = []
@@ -263,13 +278,12 @@
     ).astype(jnp.bfloat16)
     output_new = jnp.dot(hidden, params_next, preferred_element_type=jnp.float32)
     if relayed:
-        pairs = [(b, n + b) for b in range(n)] + [(n + b, b) for b in range(1, n)]
+        pairs = [(g * n + b, (1 - g) * n + b) for g in range(2) for b in range(1, n)]
         last = {(-1, 1): lax.ppermute(slices[-1], both, pairs)}
     else:
         last = exchange(slices[-1], groups)
     if relayed:
-        resid_new, returned = residual(output_new, own_target, n, 1, False, carried)
-        last = {key: value + returned for key, value in last.items()}
+        resid_new, returned = residual(output_new, own_target, n, 1, False, carried, home)
     else:
         (resid_new,) = residual(output_new, own_target, n, 1)
     other_tracker.append(last)
@@ -282,6 +296,8 @@
     base = weights[0] * tracker.astype(jnp.float32) + change / tokens
     late = lax.optimization_barrier([base[lo:hi] for lo, hi in cuts[1:]])
     gains = jnp.stack([sum(weights[o] for o in offsets) for offsets in other_tracker[0]])
+    if relayed:
+        late[-1] = late[-1] + gains[0] * returned.astype(jnp.float32)
     early = list(other_tracker[0].values())
     height = next(size for size in (10 * block, 4 * block, block) if first % size == 0)
     tracker_next = add_others(base, early, gains, height)

time: 163 us -> 208 us (1.28)
  Pallas kernels: 78.5 us -> 139 us
  waiting for transfers between devices: 40.3 us -> 20.9 us
  starting transfers between devices: 9.87 us -> 12.8 us
    pallas_call x2, Pallas kernels: 73.7 us -> 134 us  [residual(): pl.pallas_call(functools.partial(residual_kernel, z_size, lends), out_sha...]
    ppermute x4, waiting for transfers between devices: 40.3 us -> 20.9 us  [exchange(): return {(-1, 1): lax.ppermute(value, 'grp', [(0, 1), (1, 0)])}]
    ppermute x1 -> x3, starting transfers between devices: 0.79 us -> 4.4 us  [the longest x1 2.95 us: step(): beside = lax.ppermute(slices[-1][:, :width // 2], both, [(0, 1)])]
    unnamed x17 -> x19, local copies, waits for them, and re-layouts: 4.99 us -> 5 us
  transfers between devices with their start and end apart: 6 -> 8, of which waited for: 4 -> 1; matrix products, arithmetic and copies ran while one was open for 17% -> 14% of each run, Pallas kernels for 48% -> 67%
where the time goes in v2:
time: 208 us
  Pallas kernels  139 us (67%)
  waiting for transfers between devices  20.9 us (10%)
  local copies, waits for them, and re-layouts  13.9 us (7%)
  starting transfers between devices  12.8 us (6%)
  other arithmetic  10.4 us (5%)
  matrix products  9.75 us (5%)
    pallas_call x2, Pallas kernels, residual(): pl.pallas_call(functools.partial(residual_kernel, z_size, lends), out_sha...  134 us
    ppermute x4, waiting for transfers between devices, exchange(): return {(-1, 1): lax.ppermute(value, 'grp', [(0, 1), (1, 0)])}  20.9 us
    ppermute x4, starting transfers between devices, exchange(): return {(-1, 1): lax.ppermute(value, 'grp', [(0, 1), (1, 0)])}  7.77 us
    slice x4, local copies, waits for them, and re-layouts, step(): slices = [tracker[lo:hi] for lo, hi in cuts]  7.41 us
    convert_element_type x1, other arithmetic, step(): params_next = (mixed(params, other_params, weights) - step_size * tracker...  6.77 us
    unnamed x19, local copies, waits for them, and re-layouts  5 us
    pallas_call x1, Pallas kernels, add_others(): pl.pallas_call(functools.partial(add_kernel, len(others)), grid=(count,),...  4.75 us
  transfers between devices with their start and end apart: 8, of which 1 were waited for; matrix products, arithmetic and copies ran while one was open for 14% of the time, Pallas kernels for 67%

profile of v2, /device:TPU:0, one launch (start us, length us, event | category | flops | bytes accessed | tf_op | source)
XLA Modules:
  0.0 207.6 jit_solution(16045573816843300079)
XLA Ops:
  0.6 0.0 copy-start
  0.6 3.0 %collective-permute-start = (bf16[448,4096]{1,0:T(8,128)(2,1)}, bf16[448,4096]{1,0:T(8,128)(2,1)}, u32[]{:S(2)}, u32[]{:S(2)}) collective-permute-start(bf16[448,4096]{1,0:T(8,128)(2,1)} %bitcast.51), channel_id=1, source_target_pairs={{0,16},{16,0},{1,17},{17,1},{2,18},{18,2},{3,19},{19,3},{4,20},{20... | collective-permute-start | bytes 11010056 | tf_op jit(solution)/shard_map/ppermute | solution.py:35
  3.7 0.9 slice_bitcast_fusion.3.refs_0_
  4.6 0.0 copy-start.5
  4.6 0.7 collective-permute-start.7
  5.3 1.0 copy.7
  6.3 4.1 %fusion.5.part_ref = f32[4,2,2,8,4096]{4,3,2,1,0:T(8,128)} fusion(bf16[4,2,2,8,448]{4,3,2,1,0:T(8,128)(2,1)S(1)} %bitcast.56, bf16[1,448,4096]{2,1,0:T(8,128)(2,1)} %param.4), kind=kOutput, calls=%fused_computation.7 | convolution fusion | flops 469762048 | bytes 5881856 | tf_op jit(solution)/shard_map/dot_general | solution.py:260
  10.4 0.6 constant_dynamic-slice_fusion.target_ref
  11.0 39.0 %residual.2 = (bf16[4,2,2,8,4096]{4,3,2,1,0:T(8,128)(2,1)}, bf16[16,512]{1,0:T(8,128)(2,1)}) custom-call(f32[4,2,2,8,4096]{4,3,2,1,0:T(8,128)} %fusion.5.part_ref, bf16[8,4096]{1,0:T(8,128)(2,1)} %constant_dynamic-slice_fusion.target_ref, bf16[16,4096]{1,0:T(8,128)(2,1)} %copy-done.5), custom_call_target="tpu_custom_call" | custom-call | bytes 52428800 | tf_op jit(solution)/shard_map/residual/pallas_call | solution.py:199
  50.0 0.0 copy-start.3
  50.0 0.8 collective-permute-start.1
  50.8 0.8 slice.48
  51.7 2.9 %collective-permute-start.2 = (bf16[16,2048]{1,0:T(8,128)(2,1)S(1)}, bf16[16,2048]{1,0:T(8,128)(2,1)S(1)}, u32[]{:S(2)}, u32[]{:S(2)}) collective-permute-start(bf16[16,2048]{1,0:T(8,128)(2,1)S(1)} %slice.48), channel_id=1, source_target_pairs={{0,1}} | collective-permute-start | bytes 196616 | tf_op jit(solution)/shard_map/ppermute | solution.py:268
  54.6 3.5 %slice_bitcast_fusion = bf16[320,4096]{1,0:T(8,128)(2,1)} fusion(bf16[1,448,4096]{2,1,0:T(8,128)(2,1)} %param.5), kind=kLoop, calls=%fused_computation.9 | loop fusion | bytes 5242880 | tf_op jit(solution)/shard_map/slice | solution.py:259
  58.2 2.0 slice_bitcast_fusion.1
  60.2 0.9 slice_bitcast_fusion.2
  61.2 2.1 %collective-permute-start.5 = (bf16[88,4096]{1,0:T(8,128)(2,1)}, bf16[88,4096]{1,0:T(8,128)(2,1)}, u32[]{:S(2)}, u32[]{:S(2)}) collective-permute-start(bf16[88,4096]{1,0:T(8,128)(2,1)} %slice_bitcast_fusion.1), channel_id=1, source_target_pairs={{0,16},{16,0},{1,17},{17,1},{2,18},{18,2},{3,19},{19,3},{4,20},{20... | collective-permute-start | bytes 2162696 | tf_op jit(solution)/shard_map/ppermute | solution.py:35
  63.3 20.9 %collective-permute-done = bf16[448,4096]{1,0:T(8,128)(2,1)} collective-permute-done((bf16[448,4096]{1,0:T(8,128)(2,1)}, bf16[448,4096]{1,0:T(8,128)(2,1)}, u32[]{:S(2)}, u32[]{:S(2)}) %collective-permute-start) | collective-permute-done | bytes 3670048 | tf_op jit(solution)/shard_map/ppermute | solution.py:35
  84.2 0.7 collective-permute-start.3
  84.8 6.8 %fusion.2 = bf16[448,4096]{1,0:T(8,128)(2,1)S(1)} fusion(bf16[1,448,4096]{2,1,0:T(8,128)(2,1)} %param.5, bf16[448,4096]{1,0:T(8,128)(2,1)} %collective-permute-done, f32[]{:T(128)} %add.62, f32[]{:T(128)S(6)} %add.58, bf16[1,448,4096]{2,1,0:T(8,128)(2,1)} %param.4), kind=kLoop, calls=%fused_computation.4 | loop fusion | flops 16515072 | bytes 14680072 | tf_op jit(solution)/shard_map/convert_element_type | solution.py:278
  91.6 0.0 copy-start.2
  91.6 2.1 %fusion.20 = f32[4096,128]{0,1:T(8,128)} fusion(bf16[448,4096]{1,0:T(8,128)(2,1)S(1)} %fusion.2, bf16[128,448]{0,1:T(8,128)(2,1)S(1)} %copy-done.3), kind=kOutput, calls=%fused_computation.30 | convolution fusion | flops 469762048 | bytes 5881856 | tf_op jit(solution)/shard_map/dot_general | solution.py:279
  93.8 0.4 copy-done.2
  94.2 2.6 %collective-permute-start.6 = (bf16[24,4096]{1,0:T(8,128)(2,1)S(1)}, bf16[24,4096]{1,0:T(8,128)(2,1)S(1)}, u32[]{:S(2)}, u32[]{:S(2)}) collective-permute-start(bf16[24,4096]{1,0:T(8,128)(2,1)S(1)} %slice_bitcast_fusion.2), channel_id=1, source_target_pairs={{0,16},{16,0},{1,17},{17,1},{2,18},{18,2},{3,19},{19,3},{4,20},{20... | collective-permute-start | bytes 589832 | tf_op jit(solution)/shard_map/ppermute | solution.py:35
  96.8 0.6 copy-done.7
  97.4 95.2 %residual.3 = (bf16[4,2,2,8,4096]{4,3,2,1,0:T(8,128)(2,1)}, bf16[16,4096]{1,0:T(8,128)(2,1)}) custom-call(f32[4,2,2,8,4096]{4,3,2,1,0:T(8,128)} %bitcast.52, bf16[8,4096]{1,0:T(8,128)(2,1)} %constant_dynamic-slice_fusion.target_ref, bf16[16,512]{1,0:T(8,128)(2,1)} %copy-done.8, bf16[16,2048]{1,0:T(8,128)(2,1)} %copy-done.7), custom_call_target="tpu_custom_call" | custom-call | bytes 52428800 | tf_op jit(solution)/shard_map/residual/pallas_call | solution.py:199
  192.7 3.6 %fusion.4.base_ref = f32[448,4096]{1,0:T(8,128)S(1)} fusion(bf16[1,448,4096]{2,1,0:T(8,128)(2,1)} %param.5, f32[]{:T(128)S(6)} %add.58, bf16[128,4096]{1,0:T(8,128)(2,1)S(1)} %bitcast.54, bf16[128,4096]{1,0:T(8,128)(2,1)} %bitcast.55, bf16[128,448]{0,1:T(8,128)(2,1)S(1)} %neg.3, bf16[128,448]{0,1:T(8,128)(2,1)S(1)} %copy-done.3), kind=kOutput, calls=%fused_computation.6 | convolution fusion | flops 951517184 | bytes 13336580 | tf_op jit(solution)/shard_map/dot_general | solution.py:290
  196.3 2.9 %copy-done.1 = f32[448,4096]{1,0:T(8,128)} copy-done((f32[448,4096]{1,0:T(8,128)}, f32[448,4096]{1,0:T(8,128)S(1)}, u32[]{:S(2)}) %copy-start.1) | copy-done | bytes 7340056
  199.2 4.7 %add_others.1 = bf16[448,4096]{1,0:T(8,128)(2,1)} custom-call(f32[1]{0:T(128)} %bitcast.3.weights_ref, f32[448,4096]{1,0:T(8,128)} %copy-done.1, bf16[320,4096]{1,0:T(8,128)(2,1)} %collective-permute-done.4.refs_0_), custom_call_target="tpu_custom_call" | custom-call | flops 5242880 | bytes 10485760 | tf_op jit(solution)/shard_map/add_others/pallas_call | solution.py:232
  204.0 2.2 %fusion.11 = bf16[1,448,4096]{2,1,0:T(8,128)(2,1)} fusion(bf16[1,448,4096]{2,1,0:T(8,128)(2,1)} %bitcast.53, f32[88,4096]{1,0:T(8,128)S(1)} %slice-done, bf16[88,4096]{1,0:T(8,128)(2,1)} %collective-permute-done.5, f32[]{:T(128)} %add.62), kind=kLoop, calls=%fused_computation.15 | loop fusion | flops 1441792 | bytes 2884096 | tf_op jit(solution)/shard_map/dynamic_update_slice | solution.py:307
  206.2 0.7 fusion.16
  206.9 0.7 fusion.18
  (26 shorter events, 0.1 us)
Async XLA Ops:
  0.6 9.8 %copy-start = (bf16[128,4096]{1,0:T(8,128)(2,1)S(1)}, bf16[128,4096]{1,0:T(8,128)(2,1)}, u32[]{:S(2)}) copy-start(bf16[128,4096]{1,0:T(8,128)(2,1)} %param.7) | copy-start | bytes 3145732
  0.6 83.5 %collective-permute-start = (bf16[448,4096]{1,0:T(8,128)(2,1)}, bf16[448,4096]{1,0:T(8,128)(2,1)}, u32[]{:S(2)}, u32[]{:S(2)}) collective-permute-start(bf16[448,4096]{1,0:T(8,128)(2,1)} %bitcast.51), channel_id=1, source_target_pairs={{0,16},{16,0},{1,17},{17,1},{2,18},{18,2},{3,19},{19,3},{4,20},{20... | collective-permute-start | bytes 11010056 | tf_op jit(solution)/shard_map/ppermute | solution.py:35
  4.6 6.4 %copy-start.5 = (bf16[16,4096]{1,0:T(8,128)(2,1)}, bf16[16,4096]{1,0:T(8,128)(2,1)S(1)}, u32[]{:S(2)}) copy-start(bf16[16,4096]{1,0:T(8,128)(2,1)S(1)} %slice_bitcast_fusion.3.refs_0_) | copy-start | bytes 393220
  4.6 202.3 %collective-permute-start.7 = (bf16[16,4096]{1,0:T(8,128)(2,1)S(1)}, bf16[16,4096]{1,0:T(8,128)(2,1)S(1)}, u32[]{:S(2)}, u32[]{:S(2)}) collective-permute-start(bf16[16,4096]{1,0:T(8,128)(2,1)S(1)} %slice_bitcast_fusion.3.refs_0_), channel_id=1, source_target_pairs={{1,17},{2,18},{3,19},{4,20},{5,21},{6,22},{7,23},{8,24},{9,25},{10... | collective-permute-start | bytes 393224 | tf_op jit(solution)/shard_map/ppermute | solution.py:282
  50.0 11.1 %copy-start.3 = (bf16[128,448]{0,1:T(8,128)(2,1)S(1)}, bf16[128,448]{0,1:T(8,128)(2,1)}, u32[]{:S(2)}) copy-start(bf16[128,448]{0,1:T(8,128)(2,1)} %param.6) | copy-start | bytes 344068
  50.0 44.1 %collective-permute-start.1 = (bf16[16,512]{1,0:T(8,128)(2,1)}, bf16[16,512]{1,0:T(8,128)(2,1)S(1)}, u32[]{:S(2)}, u32[]{:S(2)}) collective-permute-start(bf16[16,512]{1,0:T(8,128)(2,1)} %get-tuple-element.9), channel_id=1, source_target_pairs={{9,25},{11,27},{13,29},{15,31},{17,1},{19,3},{21,5},{23,7},{25,9},... | collective-permute-start | bytes 49160 | tf_op jit(solution)/shard_map/ppermute | solution.py:270
  51.7 9.5 %collective-permute-start.2 = (bf16[16,2048]{1,0:T(8,128)(2,1)S(1)}, bf16[16,2048]{1,0:T(8,128)(2,1)S(1)}, u32[]{:S(2)}, u32[]{:S(2)}) collective-permute-start(bf16[16,2048]{1,0:T(8,128)(2,1)S(1)} %slice.48), channel_id=1, source_target_pairs={{0,1}} | collective-permute-start | bytes 196616 | tf_op jit(solution)/shard_map/ppermute | solution.py:268
  58.2 141.0 %collective-permute-start.4 = (bf16[320,4096]{1,0:T(8,128)(2,1)}, bf16[320,4096]{1,0:T(8,128)(2,1)}, u32[]{:S(2)}, u32[]{:S(2)}) collective-permute-start(bf16[320,4096]{1,0:T(8,128)(2,1)} %slice_bitcast_fusion), channel_id=1, source_target_pairs={{0,16},{16,0},{1,17},{17,1},{2,18},{18,2},{3,19},{19,3},{4,20},{20... | collective-permute-start | bytes 7864328 | tf_op jit(solution)/shard_map/ppermute | solution.py:35
  61.2 142.7 %collective-permute-start.5 = (bf16[88,4096]{1,0:T(8,128)(2,1)}, bf16[88,4096]{1,0:T(8,128)(2,1)}, u32[]{:S(2)}, u32[]{:S(2)}) collective-permute-start(bf16[88,4096]{1,0:T(8,128)(2,1)} %slice_bitcast_fusion.1), channel_id=1, source_target_pairs={{0,16},{16,0},{1,17},{17,1},{2,18},{18,2},{3,19},{19,3},{4,20},{20... | collective-permute-start | bytes 2162696 | tf_op jit(solution)/shard_map/ppermute | solution.py:35
  84.2 12.6 %collective-permute-start.3 = (bf16[16,2048]{1,0:T(8,128)(2,1)S(1)}, bf16[16,2048]{1,0:T(8,128)(2,1)S(1)}, u32[]{:S(2)}, u32[]{:S(2)}) collective-permute-start(bf16[16,2048]{1,0:T(8,128)(2,1)S(1)} %collective-permute-done.2), channel_id=1, source_target_pairs={{1,16}} | collective-permute-start | bytes 196616 | tf_op jit(solution)/shard_map/ppermute | solution.py:269
  91.6 2.5 %copy-start.2 = (bf16[448,4096]{1,0:T(8,128)(2,1)}, bf16[448,4096]{1,0:T(8,128)(2,1)S(1)}, u32[]{:S(2)}) copy-start(bf16[448,4096]{1,0:T(8,128)(2,1)S(1)} %fusion.2) | copy-start | bytes 11010052
  91.6 101.1 %copy-start.4 = (bf16[4,2,2,8,4096]{4,3,2,1,0:T(8,128)(2,1)S(1)}, bf16[4,2,2,8,4096]{4,3,2,1,0:T(8,128)(2,1)}, u32[]{:S(2)}) copy-start(bf16[4,2,2,8,4096]{4,3,2,1,0:T(8,128)(2,1)} %get-tuple-element.11) | copy-start | bytes 3145732
  94.2 2.7 %copy-start.8 = (bf16[16,512]{1,0:T(8,128)(2,1)}, bf16[16,512]{1,0:T(8,128)(2,1)S(1)}, u32[]{:S(2)}) copy-start(bf16[16,512]{1,0:T(8,128)(2,1)S(1)} %collective-permute-done.1.refs_0_) | copy-start | bytes 49156
  94.2 112.0 %collective-permute-start.6 = (bf16[24,4096]{1,0:T(8,128)(2,1)S(1)}, bf16[24,4096]{1,0:T(8,128)(2,1)S(1)}, u32[]{:S(2)}, u32[]{:S(2)}) collective-permute-start(bf16[24,4096]{1,0:T(8,128)(2,1)S(1)} %slice_bitcast_fusion.2), channel_id=1, source_target_pairs={{0,16},{16,0},{1,17},{17,1},{2,18},{18,2},{3,19},{19,3},{4,20},{20... | collective-permute-start | bytes 589832 | tf_op jit(solution)/shard_map/ppermute | solution.py:35
  96.8 0.6 copy-start.7
  196.3 2.9 %copy-start.1 = (f32[448,4096]{1,0:T(8,128)}, f32[448,4096]{1,0:T(8,128)S(1)}, u32[]{:S(2)}) copy-start(f32[448,4096]{1,0:T(8,128)S(1)} %fusion.4.base_ref) | copy-start | bytes 22020100
  199.2 4.8 %slice-start = ((f32[448,4096]{1,0:T(8,128)}), f32[88,4096]{1,0:T(8,128)S(1)}, s32[]{:S(2)}) async-start(f32[448,4096]{1,0:T(8,128)} %copy-done.1), calls=%async_computation | async-start | bytes 2883584 | tf_op jit(solution)/shard_map/slice | solution.py:297
  199.2 7.0 %slice-start.1 = ((f32[448,4096]{1,0:T(8,128)}), f32[24,4096]{1,0:T(8,128)S(1)}, s32[]{:S(2)}) async-start(f32[448,4096]{1,0:T(8,128)} %copy-done.1), calls=%async_computation.1 | async-start | bytes 786432 | tf_op jit(solution)/shard_map/slice | solution.py:297
  204.0 3.0 %slice-start.2 = ((f32[448,4096]{1,0:T(8,128)}), f32[16,4096]{1,0:T(8,128)S(1)}, s32[]{:S(2)}) async-start(f32[448,4096]{1,0:T(8,128)} %copy-done.1), calls=%async_computation.2 | async-start | bytes 524288 | tf_op jit(solution)/shard_map/slice | solution.py:297
  204.0 3.0 %copy-start.6 = (bf16[16,4096]{1,0:T(8,128)(2,1)S(1)}, bf16[16,4096]{1,0:T(8,128)(2,1)}, u32[]{:S(2)}) copy-start(bf16[16,4096]{1,0:T(8,128)(2,1)} %get-tuple-element.15) | copy-start | bytes 393220

commit v3 on v1

--- a/solution.py
+++ b/solution.py
@@ -42,7 +42,7 @@
 
 
 def helpers(z_size):
-    return [3] + [4 * z + 1 for z in range(1, z_size)]
+    return [2 * chip + 1 for chip in range(2 * z_size)]
 
 
 def mixed(own, others, weights):
@@ -76,7 +76,8 @@
     greeted = [core_peer, y_peer, *z_peers]
     if lends is not None:
         relay_s, relay_r = sems[12:]
-        greeted += [z * 4 + (1 - y) * 2 + 1 - c, *[spot * 4 + y * 2 + 1 - c for spot in z_spots]]
+        greeted += [spot * 4 + y * 2 + 1 - c for spot in z_spots]
+        greeted += [spot * 4 + (1 - y) * 2 + 1 - c for spot in [z, *z_spots]]
         home = (lax.axis_index("grp") == (1 if lends else 0)) & (me == 0)
         helps = [
             (lax.axis_index("grp") == (1 if lends else 0)) & (me == spot) for spot in helpers(z_size)
@@ -93,7 +94,7 @@
     pl.semaphore_wait(barrier, len(greeted))
 
     def relay(j):
-        length = target_ref.shape[-1] // z_size
+        length = target_ref.shape[-1] // (2 * z_size)
         at = pl.ds(j * length, length)
         return pltpu.make_async_remote_copy(
             src_ref=near_ref.at[:, at] if lends else near_ref,
@@ -105,7 +106,7 @@
         )
 
     def relay_all(act):
-        for j in range(z_size):
+        for j in range(2 * z_size):
             pl.when(home if lends else helps[j])(functools.partial(act, j))
 
     if lends is not None:
@@ -167,7 +168,7 @@
     for copy in give_core:
         copy.wait_recv()
     if lends is not None:
-        for j in range(z_size):
+        for j in range(2 * z_size):
             pl.when(helps[j] if lends else home)(lambda j=j: relay(j).wait_recv())
         relay_all(lambda j: relay(j).wait_send())
     for copy in [*over_core, *over_y, *sum(over_z, []), *sum(give_z, []), *give_y, *give_core]:
@@ -184,7 +185,7 @@
     operands = [output.reshape(z_size, 2, 2, share, width), own_target]
     if lends is not None:
         operands.append(near)
-        wide = width // z_size if lends else width
+        wide = width // (2 * z_size) if lends else width
         shapes.append(jax.ShapeDtypeStruct((near.shape[0], wide), near.dtype))
     resid, *far = pl.pallas_call(
         functools.partial(residual_kernel, z_size, lends),
@@ -198,7 +199,7 @@
             pltpu.VMEM((z_size, share, width), jnp.float32),
             pltpu.VMEM((z_size - 1, share, width), jnp.float32),
             one, one, one, one, many, many, many, many, one, one, one, one,
-            *([] if lends is None else [pltpu.SemaphoreType.DMA((z_size,))] * 2),
+            *([] if lends is None else [pltpu.SemaphoreType.DMA((2 * z_size,))] * 2),
         ],
         compiler_params=pltpu.CompilerParams(collective_id=which, has_side_effects=True),
         cost_estimate=pl.CostEstimate(flops=0, bytes_accessed=100 * tokens * width, transcendentals=0),
@@ -242,8 +243,8 @@
     params, tracker = params[0], tracker[0]
     rows = params.shape[0]
     block = 16
-    first = rows * 5 // 7 // 16 * 16
-    ends = sorted({first, max(first, rows - 40), max(first, rows - 16), rows})
+    first = rows * 6 // 7 // 16 * 16
+    ends = sorted({first, max(first, rows - 16), rows})
     cuts = list(zip([0, *ends[:-1]], ends))
     other_params = exchange(params, groups)
     slices = [tracker[lo:hi] for lo, hi in cuts]
@@ -252,6 +253,8 @@
     if relayed:
         resid_old, lent = residual(output_old, own_target, n, 0, True, slices[-1])
         both, spots = ("grp", "blk"), helpers(n // 4)
+        beside = lax.ppermute(slices[-1], both, [(0, 1)])
+        home = lax.ppermute(beside, both, [(1, n)])
         carried = lax.ppermute(lent, both, [(n + spot, spot) for spot in spots])
     else:
         (resid_old,) = residual(output_old, own_target, n, 0)
@@ -263,13 +266,12 @@
     ).astype(jnp.bfloat16)
     output_new = jnp.dot(hidden, params_next, preferred_element_type=jnp.float32)
     if relayed:
-        pairs = [(b, n + b) for b in range(n)] + [(n + b, b) for b in range(1, n)]
+        pairs = [(g * n + b, (1 - g) * n + b) for g in range(2) for b in range(1, n)]
         last = {(-1, 1): lax.ppermute(slices[-1], both, pairs)}
     else:
         last = exchange(slices[-1], groups)
     if relayed:
         resid_new, returned = residual(output_new, own_target, n, 1, False, carried)
-        last = {key: value + returned for key, value in last.items()}
     else:
         (resid_new,) = residual(output_new, own_target, n, 1)
     other_tracker.append(last)
@@ -282,6 +284,8 @@
     base = weights[0] * tracker.astype(jnp.float32) + change / tokens
     late = lax.optimization_barrier([base[lo:hi] for lo, hi in cuts[1:]])
     gains = jnp.stack([sum(weights[o] for o in offsets) for offsets in other_tracker[0]])
+    if relayed:
+        late[-1] = late[-1] + gains[0] * (home + returned).astype(jnp.float32)
     early = list(other_tracker[0].values())
     height = next(size for size in (10 * block, 4 * block, block) if first % size == 0)
     tracker_next = add_others(base, early, gains, height)

time: 163 us -> 206 us (1.26)
  Pallas kernels: 78.5 us -> 140 us
  waiting for transfers between devices: 40.3 us -> 25.4 us
  local copies, waits for them, and re-layouts: 13 us -> 10.5 us
    pallas_call x2, Pallas kernels: 73.7 us -> 133 us  [residual(): pl.pallas_call(functools.partial(residual_kernel, z_size, lends), out_sha...]
    ppermute x4 -> x3, waiting for transfers between devices: 40.3 us -> 25.4 us  [exchange(): return {(-1, 1): lax.ppermute(value, 'grp', [(0, 1), (1, 0)])}]
    ppermute x0 -> x2, starting transfers between devices: none -> 4.11 us  [the longest x1 3.45 us: step(): beside = lax.ppermute(slices[-1], both, [(0, 1)])]
    ppermute x4 -> x3, starting transfers between devices: 7.07 us -> 4.34 us  [exchange(): return {(-1, 1): lax.ppermute(value, 'grp', [(0, 1), (1, 0)])}]
    slice x4 -> x3, local copies, waits for them, and re-layouts: 7.43 us -> 5.84 us  [step(): slices = [tracker[lo:hi] for lo, hi in cuts]]
    unnamed x17 -> x15, local copies, waits for them, and re-layouts: 4.99 us -> 4.07 us
  transfers between devices with their start and end apart: 6 -> 7, of which waited for: 4 -> 1; matrix products, arithmetic and copies ran while one was open for 17% -> 12% of each run, Pallas kernels for 48% -> 68%
where the time goes in v3:
time: 206 us
  Pallas kernels  140 us (68%)
  waiting for transfers between devices  25.4 us (12%)
  local copies, waits for them, and re-layouts  10.5 us (5%)
  starting transfers between devices  9.78 us (5%)
  matrix products  9.75 us (5%)
  other arithmetic  9.28 us (5%)
    pallas_call x2, Pallas kernels, residual(): pl.pallas_call(functools.partial(residual_kernel, z_size, lends), out_sha...  133 us
    ppermute x3, waiting for transfers between devices, exchange(): return {(-1, 1): lax.ppermute(value, 'grp', [(0, 1), (1, 0)])}  25.4 us
    convert_element_type x1, other arithmetic, step(): params_next = (mixed(params, other_params, weights) - step_size * tracker...  6.77 us
    pallas_call x1, Pallas kernels, add_others(): pl.pallas_call(functools.partial(add_kernel, len(others)), grid=(count,),...  6.74 us
    slice x3, local copies, waits for them, and re-layouts, step(): slices = [tracker[lo:hi] for lo, hi in cuts]  5.84 us
    ppermute x3, starting transfers between devices, exchange(): return {(-1, 1): lax.ppermute(value, 'grp', [(0, 1), (1, 0)])}  4.34 us
  transfers between devices with their start and end apart: 7, of which 1 were waited for; matrix products, arithmetic and copies ran while one was open for 12% of the time, Pallas kernels for 68%

profile of v3, /device:TPU:0, one launch (start us, length us, event | category | flops | bytes accessed | tf_op | source)
XLA Modules:
  0.0 205.7 jit_solution(16732636988963566899)
XLA Ops:
  0.6 0.0 copy-start
  0.7 3.0 %collective-permute-start = (bf16[448,4096]{1,0:T(8,128)(2,1)}, bf16[448,4096]{1,0:T(8,128)(2,1)}, u32[]{:S(2)}, u32[]{:S(2)}) collective-permute-start(bf16[448,4096]{1,0:T(8,128)(2,1)} %bitcast.45), channel_id=1, source_target_pairs={{0,16},{16,0},{1,17},{17,1},{2,18},{18,2},{3,19},{19,3},{4,20},{20... | collective-permute-start | bytes 11010056 | tf_op jit(solution)/shard_map/ppermute | solution.py:35
  3.7 0.9 slice_bitcast_fusion.2.refs_0_
  4.6 0.7 collective-permute-start.6
  5.3 3.4 %collective-permute-start.4 = (bf16[16,4096]{1,0:T(8,128)(2,1)S(1)}, bf16[16,4096]{1,0:T(8,128)(2,1)}, u32[]{:S(2)}, u32[]{:S(2)}) collective-permute-start(bf16[16,4096]{1,0:T(8,128)(2,1)S(1)} %slice_bitcast_fusion.2.refs_0_), channel_id=1, source_target_pairs={{0,1}} | collective-permute-start | bytes 393224 | tf_op jit(solution)/shard_map/ppermute | solution.py:256
  8.7 3.9 %slice_bitcast_fusion = bf16[384,4096]{1,0:T(8,128)(2,1)} fusion(bf16[1,448,4096]{2,1,0:T(8,128)(2,1)} %param.5), kind=kLoop, calls=%fused_computation.9 | loop fusion | bytes 6291456 | tf_op jit(solution)/shard_map/slice | solution.py:250
  12.6 0.0 collective-permute-start.2
  12.7 0.1 copy.7
  12.8 0.6 constant_dynamic-slice_fusion.target_ref
  13.4 4.1 %fusion.5.part_ref = f32[4,2,2,8,4096]{4,3,2,1,0:T(8,128)} fusion(bf16[4,2,2,8,448]{4,3,2,1,0:T(8,128)(2,1)S(1)} %bitcast.50, bf16[1,448,4096]{2,1,0:T(8,128)(2,1)} %param.4), kind=kOutput, calls=%fused_computation.7 | convolution fusion | flops 469762048 | bytes 5881856 | tf_op jit(solution)/shard_map/dot_general | solution.py:251
  17.5 38.2 %residual.2 = (bf16[4,2,2,8,4096]{4,3,2,1,0:T(8,128)(2,1)}, bf16[16,512]{1,0:T(8,128)(2,1)}) custom-call(f32[4,2,2,8,4096]{4,3,2,1,0:T(8,128)} %fusion.5.part_ref, bf16[8,4096]{1,0:T(8,128)(2,1)} %constant_dynamic-slice_fusion.target_ref, bf16[16,4096]{1,0:T(8,128)(2,1)} %copy-done.5), custom_call_target="tpu_custom_call" | custom-call | bytes 52428800 | tf_op jit(solution)/shard_map/residual/pallas_call | solution.py:190
  55.7 0.7 collective-permute-start.1
  56.4 1.0 slice_bitcast_fusion.1
  57.5 0.0 collective-permute-done.4
  57.5 1.3 collective-permute-start.3
  58.8 25.4 %collective-permute-done = bf16[448,4096]{1,0:T(8,128)(2,1)} collective-permute-done((bf16[448,4096]{1,0:T(8,128)(2,1)}, bf16[448,4096]{1,0:T(8,128)(2,1)}, u32[]{:S(2)}, u32[]{:S(2)}) %collective-permute-start) | collective-permute-done | bytes 3670048 | tf_op jit(solution)/shard_map/ppermute | solution.py:35
  84.2 0.7 collective-permute-start.5
  84.9 6.8 %fusion.2 = bf16[448,4096]{1,0:T(8,128)(2,1)S(1)} fusion(bf16[1,448,4096]{2,1,0:T(8,128)(2,1)} %param.5, bf16[448,4096]{1,0:T(8,128)(2,1)} %collective-permute-done, f32[]{:T(128)} %add.62, f32[]{:T(128)S(6)} %add.58, bf16[1,448,4096]{2,1,0:T(8,128)(2,1)} %param.4), kind=kLoop, calls=%fused_computation.4 | loop fusion | flops 16515072 | bytes 14680072 | tf_op jit(solution)/shard_map/convert_element_type | solution.py:266
  91.6 0.0 copy-start.2
  91.7 2.1 %fusion.18 = f32[4096,128]{0,1:T(8,128)} fusion(bf16[448,4096]{1,0:T(8,128)(2,1)S(1)} %fusion.2, bf16[128,448]{0,1:T(8,128)(2,1)S(1)} %copy-done.3), kind=kOutput, calls=%fused_computation.26 | convolution fusion | flops 469762048 | bytes 5881856 | tf_op jit(solution)/shard_map/dot_general | solution.py:267
  93.8 0.4 copy-done.2
  94.2 0.0 collective-permute-done.1.refs_0_
  94.2 0.6 copy-done.6
  94.8 95.2 %residual.3 = (bf16[4,2,2,8,4096]{4,3,2,1,0:T(8,128)(2,1)}, bf16[16,4096]{1,0:T(8,128)(2,1)}) custom-call(f32[4,2,2,8,4096]{4,3,2,1,0:T(8,128)} %bitcast.46, bf16[8,4096]{1,0:T(8,128)(2,1)} %constant_dynamic-slice_fusion.target_ref, bf16[16,512]{1,0:T(8,128)(2,1)} %copy-done.6), custom_call_target="tpu_custom_call" | custom-call | bytes 52428800 | tf_op jit(solution)/shard_map/residual/pallas_call | solution.py:190
  190.0 3.6 %fusion.4.base_ref = f32[448,4096]{1,0:T(8,128)S(1)} fusion(bf16[1,448,4096]{2,1,0:T(8,128)(2,1)} %param.5, f32[]{:T(128)S(6)} %add.58, bf16[128,4096]{1,0:T(8,128)(2,1)S(1)} %bitcast.48, bf16[128,4096]{1,0:T(8,128)(2,1)} %bitcast.49, bf16[128,448]{0,1:T(8,128)(2,1)S(1)} %neg.3, bf16[128,448]{0,1:T(8,128)(2,1)S(1)} %copy-done.3), kind=kOutput, calls=%fused_computation.6 | convolution fusion | flops 951517184 | bytes 13336580 | tf_op jit(solution)/shard_map/dot_general | solution.py:278
  193.5 2.9 %copy-done.1 = f32[448,4096]{1,0:T(8,128)} copy-done((f32[448,4096]{1,0:T(8,128)}, f32[448,4096]{1,0:T(8,128)S(1)}, u32[]{:S(2)}) %copy-start.1) | copy-done | bytes 7340056
  196.5 0.0 collective-permute-done.2.refs_0_
  196.5 6.7 %add_others.1 = bf16[448,4096]{1,0:T(8,128)(2,1)} custom-call(f32[1]{0:T(128)} %bitcast.3.weights_ref, f32[448,4096]{1,0:T(8,128)} %copy-done.1, bf16[384,4096]{1,0:T(8,128)(2,1)} %collective-permute-done.2.refs_0_), custom_call_target="tpu_custom_call" | custom-call | flops 6291456 | bytes 12582912 | tf_op jit(solution)/shard_map/add_others/pallas_call | solution.py:223
  203.2 0.0 collective-permute-done.3
  203.2 0.8 fusion.11
  204.1 0.0 collective-permute-done.6
  204.1 1.6 fusion.16
  (15 shorter events, 0.1 us)
Async XLA Ops:
  0.6 12.1 %copy-start = (bf16[128,4096]{1,0:T(8,128)(2,1)S(1)}, bf16[128,4096]{1,0:T(8,128)(2,1)}, u32[]{:S(2)}) copy-start(bf16[128,4096]{1,0:T(8,128)(2,1)} %param.7) | copy-start | bytes 3145732
  0.6 12.0 %copy-start.3 = (bf16[128,448]{0,1:T(8,128)(2,1)S(1)}, bf16[128,448]{0,1:T(8,128)(2,1)}, u32[]{:S(2)}) copy-start(bf16[128,448]{0,1:T(8,128)(2,1)} %param.6) | copy-start | bytes 344068
  0.7 83.5 %collective-permute-start = (bf16[448,4096]{1,0:T(8,128)(2,1)}, bf16[448,4096]{1,0:T(8,128)(2,1)}, u32[]{:S(2)}, u32[]{:S(2)}) collective-permute-start(bf16[448,4096]{1,0:T(8,128)(2,1)} %bitcast.45), channel_id=1, source_target_pairs={{0,16},{16,0},{1,17},{17,1},{2,18},{18,2},{3,19},{19,3},{4,20},{20... | collective-permute-start | bytes 11010056 | tf_op jit(solution)/shard_map/ppermute | solution.py:35
  4.6 12.9 %copy-start.5 = (bf16[16,4096]{1,0:T(8,128)(2,1)}, bf16[16,4096]{1,0:T(8,128)(2,1)S(1)}, u32[]{:S(2)}) copy-start(bf16[16,4096]{1,0:T(8,128)(2,1)S(1)} %slice_bitcast_fusion.2.refs_0_) | copy-start | bytes 393220
  4.6 199.5 %collective-permute-start.6 = (bf16[16,4096]{1,0:T(8,128)(2,1)S(1)}, bf16[16,4096]{1,0:T(8,128)(2,1)S(1)}, u32[]{:S(2)}, u32[]{:S(2)}) collective-permute-start(bf16[16,4096]{1,0:T(8,128)(2,1)S(1)} %slice_bitcast_fusion.2.refs_0_), channel_id=1, source_target_pairs={{1,17},{2,18},{3,19},{4,20},{5,21},{6,22},{7,23},{8,24},{9,25},{10... | collective-permute-start | bytes 393224 | tf_op jit(solution)/shard_map/ppermute | solution.py:270
  5.3 52.2 %collective-permute-start.4 = (bf16[16,4096]{1,0:T(8,128)(2,1)S(1)}, bf16[16,4096]{1,0:T(8,128)(2,1)}, u32[]{:S(2)}, u32[]{:S(2)}) collective-permute-start(bf16[16,4096]{1,0:T(8,128)(2,1)S(1)} %slice_bitcast_fusion.2.refs_0_), channel_id=1, source_target_pairs={{0,1}} | collective-permute-start | bytes 393224 | tf_op jit(solution)/shard_map/ppermute | solution.py:256
  12.6 183.8 %collective-permute-start.2 = (bf16[384,4096]{1,0:T(8,128)(2,1)}, bf16[384,4096]{1,0:T(8,128)(2,1)}, u32[]{:S(2)}, u32[]{:S(2)}) collective-permute-start(bf16[384,4096]{1,0:T(8,128)(2,1)} %slice_bitcast_fusion), channel_id=1, source_target_pairs={{0,16},{16,0},{1,17},{17,1},{2,18},{18,2},{3,19},{19,3},{4,20},{20... | collective-permute-start | bytes 9437192 | tf_op jit(solution)/shard_map/ppermute | solution.py:35
  55.7 38.4 %collective-permute-start.1 = (bf16[16,512]{1,0:T(8,128)(2,1)}, bf16[16,512]{1,0:T(8,128)(2,1)S(1)}, u32[]{:S(2)}, u32[]{:S(2)}) collective-permute-start(bf16[16,512]{1,0:T(8,128)(2,1)} %get-tuple-element.8), channel_id=1, source_target_pairs={{17,1},{19,3},{21,5},{23,7},{25,9},{27,11},{29,13},{31,15}} | collective-permute-start | bytes 49160 | tf_op jit(solution)/shard_map/ppermute | solution.py:258
  57.5 145.7 %collective-permute-start.3 = (bf16[48,4096]{1,0:T(8,128)(2,1)S(1)}, bf16[48,4096]{1,0:T(8,128)(2,1)S(1)}, u32[]{:S(2)}, u32[]{:S(2)}) collective-permute-start(bf16[48,4096]{1,0:T(8,128)(2,1)S(1)} %slice_bitcast_fusion.1), channel_id=1, source_target_pairs={{0,16},{16,0},{1,17},{17,1},{2,18},{18,2},{3,19},{19,3},{4,20},{20... | collective-permute-start | bytes 1179656 | tf_op jit(solution)/shard_map/ppermute | solution.py:35
  84.2 119.9 %collective-permute-start.5 = (bf16[16,4096]{1,0:T(8,128)(2,1)}, bf16[16,4096]{1,0:T(8,128)(2,1)S(1)}, u32[]{:S(2)}, u32[]{:S(2)}) collective-permute-start(bf16[16,4096]{1,0:T(8,128)(2,1)} %collective-permute-done.4), channel_id=1, source_target_pairs={{1,16}} | collective-permute-start | bytes 393224 | tf_op jit(solution)/shard_map/ppermute | solution.py:257
  91.6 2.5 %copy-start.2 = (bf16[448,4096]{1,0:T(8,128)(2,1)}, bf16[448,4096]{1,0:T(8,128)(2,1)S(1)}, u32[]{:S(2)}) copy-start(bf16[448,4096]{1,0:T(8,128)(2,1)S(1)} %fusion.2) | copy-start | bytes 11010052
  91.6 98.3 %copy-start.4 = (bf16[4,2,2,8,4096]{4,3,2,1,0:T(8,128)(2,1)S(1)}, bf16[4,2,2,8,4096]{4,3,2,1,0:T(8,128)(2,1)}, u32[]{:S(2)}) copy-start(bf16[4,2,2,8,4096]{4,3,2,1,0:T(8,128)(2,1)} %get-tuple-element.10) | copy-start | bytes 3145732
  94.2 0.6 copy-start.6
  193.5 2.9 %copy-start.1 = (f32[448,4096]{1,0:T(8,128)}, f32[448,4096]{1,0:T(8,128)S(1)}, u32[]{:S(2)}) copy-start(f32[448,4096]{1,0:T(8,128)S(1)} %fusion.4.base_ref) | copy-start | bytes 22020100
  196.5 6.8 %slice-start = ((f32[448,4096]{1,0:T(8,128)}), f32[48,4096]{1,0:T(8,128)S(1)}, s32[]{:S(2)}) async-start(f32[448,4096]{1,0:T(8,128)} %copy-done.1), calls=%async_computation | async-start | bytes 1572864 | tf_op jit(solution)/shard_map/slice | solution.py:285
  196.5 7.6 %slice-start.1 = ((f32[448,4096]{1,0:T(8,128)}), f32[16,4096]{1,0:T(8,128)S(1)}, s32[]{:S(2)}) async-start(f32[448,4096]{1,0:T(8,128)} %copy-done.1), calls=%async_computation.1 | async-start | bytes 524288 | tf_op jit(solution)/shard_map/slice | solution.py:285

commit v4 on v2

--- a/solution.py
+++ b/solution.py
@@ -82,7 +82,7 @@
         greeted += [spot * 4 + (1 - y) * 2 + 1 - c for spot in [z, *z_spots]]
         length = target_ref.shape[-1] // (2 * z_size)
         late_side = lax.axis_index("grp") == (1 if lends else 0)
-        travels = [late_side | (j >= z_size) for j in range(2 * z_size)]
+        travels = [late_side for _ in range(2 * z_size)]
         homes = [(me == 0) & travel for travel in travels]
         helps = [(me == spot) & travel for spot, travel in zip(helpers(z_size), travels)]
         if lends:
@@ -93,7 +93,7 @@
 
             @pl.when(jnp.logical_not(filled))
             def _(at=at):
-                if lends or at.start >= home_ref.shape[-1]:
+                if lends:
                     far_ref[:, at] = jnp.zeros((far_ref.shape[0], length), far_ref.dtype)
                 else:
                     far_ref[:, at] = home_ref[:, at]
@@ -263,11 +263,9 @@
         resid_old, lent = residual(output_old, own_target, n, 0, True, slices[-1])
         both, spots = ("grp", "blk"), helpers(n // 4)
         inward = [(n + spot, spot) for spot in spots]
-        outward = [(spot, n + spot) for spot in spots[len(spots) // 2 :]]
-        width = params.shape[1]
-        beside = lax.ppermute(slices[-1][:, : width // 2], both, [(0, 1)])
+        beside = lax.ppermute(slices[-1], both, [(0, 1)])
         home = lax.ppermute(beside, both, [(1, n)])
-        carried = lax.ppermute(lent, both, outward + inward)
+        carried = lax.ppermute(lent, both, inward)
     else:
         (resid_old,) = residual(output_old, own_target, n, 0)
     other_tracker = []

time: 208 us -> 214 us (1.029)
  waiting for transfers between devices: 20.9 us -> 27 us
  Pallas kernels: 139 us -> 142 us
  starting transfers between devices: 12.8 us -> 9.94 us
    ppermute x4, waiting for transfers between devices: 20.9 us -> 27 us  [exchange(): return {(-1, 1): lax.ppermute(value, 'grp', [(0, 1), (1, 0)])}]
    pallas_call x2, Pallas kernels: 134 us -> 137 us  [residual(): pl.pallas_call(functools.partial(residual_kernel, z_size, lends), out_sha...]
    ppermute x4, starting transfers between devices: 7.77 us -> 5.42 us  [exchange(): return {(-1, 1): lax.ppermute(value, 'grp', [(0, 1), (1, 0)])}]
  transfers between devices with their start and end apart: 8 -> 8, of which waited for: 1 -> 1; matrix products, arithmetic and copies ran while one was open for 14% -> 13% of each run, Pallas kernels for 67% -> 67%
where the time goes in v4:
time: 214 us; the launch traced here: 213 us
  Pallas kernels  142 us (66%)
  waiting for transfers between devices  27 us (13%)
  local copies, waits for them, and re-layouts  13.2 us (6%)
  other arithmetic  10.4 us (5%)
  starting transfers between devices  9.94 us (5%)
  matrix products  9.74 us (5%)
    pallas_call x2, Pallas kernels, residual(): pl.pallas_call(functools.partial(residual_kernel, z_size, lends), out_sha...  137 us
    ppermute x4, waiting for transfers between devices, exchange(): return {(-1, 1): lax.ppermute(value, 'grp', [(0, 1), (1, 0)])}  27 us
    slice x4, local copies, waits for them, and re-layouts, step(): slices = [tracker[lo:hi] for lo, hi in cuts]  7.5 us
    convert_element_type x1, other arithmetic, step(): params_next = (mixed(params, other_params, weights) - step_size * tracker...  6.77 us
    ppermute x4, starting transfers between devices, exchange(): return {(-1, 1): lax.ppermute(value, 'grp', [(0, 1), (1, 0)])}  5.42 us
    unnamed x19, local copies, waits for them, and re-layouts  5.02 us
    pallas_call x1, Pallas kernels, add_others(): pl.pallas_call(functools.partial(add_kernel, len(others)), grid=(count,),...  4.75 us
  transfers between devices with their start and end apart: 8, of which 1 were waited for; matrix products, arithmetic and copies ran while one was open for 13% of the time, Pallas kernels for 67%

profile of v4, /device:TPU:0, one launch (start us, length us, event | category | flops | bytes accessed | tf_op | source)
XLA Modules:
  0.0 212.8 jit_solution(15167864311793975179)
XLA Ops:
  0.6 0.0 copy-start
  0.6 1.0 slice_bitcast_fusion.3.refs_0_
  1.7 0.0 copy-start.5
  1.7 2.4 %collective-permute-start.2 = (bf16[16,4096]{1,0:T(8,128)(2,1)S(1)}, bf16[16,4096]{1,0:T(8,128)(2,1)S(1)}, u32[]{:S(2)}, u32[]{:S(2)}) collective-permute-start(bf16[16,4096]{1,0:T(8,128)(2,1)S(1)} %slice_bitcast_fusion.3.refs_0_), channel_id=1, source_target_pairs={{0,1}} | collective-permute-start | bytes 393224 | tf_op jit(solution)/shard_map/ppermute | solution.py:266
  4.1 0.7 collective-permute-start.7
  4.8 1.3 collective-permute-start
  6.0 1.0 copy.7
  7.1 4.1 %fusion.5.part_ref = f32[4,2,2,8,4096]{4,3,2,1,0:T(8,128)} fusion(bf16[4,2,2,8,448]{4,3,2,1,0:T(8,128)(2,1)S(1)} %bitcast.56, bf16[1,448,4096]{2,1,0:T(8,128)(2,1)} %param.4), kind=kOutput, calls=%fused_computation.7 | convolution fusion | flops 469762048 | bytes 5881856 | tf_op jit(solution)/shard_map/dot_general | solution.py:260
  11.1 0.6 constant_dynamic-slice_fusion.target_ref
  11.8 38.9 %residual.2 = (bf16[4,2,2,8,4096]{4,3,2,1,0:T(8,128)(2,1)}, bf16[16,512]{1,0:T(8,128)(2,1)}) custom-call(f32[4,2,2,8,4096]{4,3,2,1,0:T(8,128)} %fusion.5.part_ref, bf16[8,4096]{1,0:T(8,128)(2,1)} %constant_dynamic-slice_fusion.target_ref, bf16[16,4096]{1,0:T(8,128)(2,1)} %copy-done.5), custom_call_target="tpu_custom_call" | custom-call | bytes 52428800 | tf_op jit(solution)/shard_map/residual/pallas_call | solution.py:199
  50.7 0.0 copy-start.3
  50.7 0.8 collective-permute-start.1
  51.5 3.5 %slice_bitcast_fusion = bf16[320,4096]{1,0:T(8,128)(2,1)} fusion(bf16[1,448,4096]{2,1,0:T(8,128)(2,1)} %param.5), kind=kLoop, calls=%fused_computation.9 | loop fusion | bytes 5242880 | tf_op jit(solution)/shard_map/slice | solution.py:259
  55.0 2.2 %collective-permute-start.4 = (bf16[320,4096]{1,0:T(8,128)(2,1)}, bf16[320,4096]{1,0:T(8,128)(2,1)}, u32[]{:S(2)}, u32[]{:S(2)}) collective-permute-start(bf16[320,4096]{1,0:T(8,128)(2,1)} %slice_bitcast_fusion), channel_id=1, source_target_pairs={{0,16},{16,0},{1,17},{17,1},{2,18},{18,2},{3,19},{19,3},{4,20},{20... | collective-permute-start | bytes 7864328 | tf_op jit(solution)/shard_map/ppermute | solution.py:35
  57.2 2.0 slice_bitcast_fusion.1
  59.3 0.9 slice_bitcast_fusion.2
  60.3 0.1 collective-permute-start.5
  60.4 27.0 %collective-permute-done = bf16[448,4096]{1,0:T(8,128)(2,1)} collective-permute-done((bf16[448,4096]{1,0:T(8,128)(2,1)}, bf16[448,4096]{1,0:T(8,128)(2,1)}, u32[]{:S(2)}, u32[]{:S(2)}) %collective-permute-start) | collective-permute-done | bytes 3670048 | tf_op jit(solution)/shard_map/ppermute | solution.py:35
  87.3 0.7 collective-permute-start.3
  88.0 6.8 %fusion.2 = bf16[448,4096]{1,0:T(8,128)(2,1)S(1)} fusion(bf16[1,448,4096]{2,1,0:T(8,128)(2,1)} %param.5, bf16[448,4096]{1,0:T(8,128)(2,1)} %collective-permute-done, f32[]{:T(128)} %add.62, f32[]{:T(128)S(6)} %add.58, bf16[1,448,4096]{2,1,0:T(8,128)(2,1)} %param.4), kind=kLoop, calls=%fused_computation.4 | loop fusion | flops 16515072 | bytes 14680072 | tf_op jit(solution)/shard_map/convert_element_type | solution.py:276
  94.8 0.0 copy-start.2
  94.8 2.1 fusion.20
  96.9 0.4 copy-done.2
  97.3 1.9 collective-permute-start.6
  99.2 0.6 copy-done.6
  99.8 98.0 %residual.3 = (bf16[4,2,2,8,4096]{4,3,2,1,0:T(8,128)(2,1)}, bf16[16,4096]{1,0:T(8,128)(2,1)}) custom-call(f32[4,2,2,8,4096]{4,3,2,1,0:T(8,128)} %bitcast.52, bf16[8,4096]{1,0:T(8,128)(2,1)} %constant_dynamic-slice_fusion.target_ref, bf16[16,512]{1,0:T(8,128)(2,1)} %copy-done.8, bf16[16,4096]{1,0:T(8,128)(2,1)} %copy-done.6), custom_call_target="tpu_custom_call" | custom-call | bytes 52428800 | tf_op jit(solution)/shard_map/residual/pallas_call | solution.py:199
  197.9 3.6 %fusion.4.base_ref = f32[448,4096]{1,0:T(8,128)S(1)} fusion(bf16[1,448,4096]{2,1,0:T(8,128)(2,1)} %param.5, f32[]{:T(128)S(6)} %add.58, bf16[128,4096]{1,0:T(8,128)(2,1)S(1)} %bitcast.54, bf16[128,4096]{1,0:T(8,128)(2,1)} %bitcast.55, bf16[128,448]{0,1:T(8,128)(2,1)S(1)} %neg.3, bf16[128,448]{0,1:T(8,128)(2,1)S(1)} %copy-done.3), kind=kOutput, calls=%fused_computation.6 | convolution fusion | flops 951517184 | bytes 13336580 | tf_op jit(solution)/shard_map/dot_general | solution.py:288
  201.4 2.9 %copy-done.1 = f32[448,4096]{1,0:T(8,128)} copy-done((f32[448,4096]{1,0:T(8,128)}, f32[448,4096]{1,0:T(8,128)S(1)}, u32[]{:S(2)}) %copy-start.1) | copy-done | bytes 7340056
  204.4 4.7 %add_others.1 = bf16[448,4096]{1,0:T(8,128)(2,1)} custom-call(f32[1]{0:T(128)} %bitcast.3.weights_ref, f32[448,4096]{1,0:T(8,128)} %copy-done.1, bf16[320,4096]{1,0:T(8,128)(2,1)} %collective-permute-done.4.refs_0_), custom_call_target="tpu_custom_call" | custom-call | flops 5242880 | bytes 10485760 | tf_op jit(solution)/shard_map/add_others/pallas_call | solution.py:232
  209.1 2.2 %fusion.11 = bf16[1,448,4096]{2,1,0:T(8,128)(2,1)} fusion(bf16[1,448,4096]{2,1,0:T(8,128)(2,1)} %bitcast.53, f32[88,4096]{1,0:T(8,128)S(1)} %slice-done, bf16[88,4096]{1,0:T(8,128)(2,1)} %collective-permute-done.5, f32[]{:T(128)} %add.62), kind=kLoop, calls=%fused_computation.15 | loop fusion | flops 1441792 | bytes 2884096 | tf_op jit(solution)/shard_map/dynamic_update_slice | solution.py:305
  211.3 0.7 fusion.16
  212.1 0.7 fusion.18
  (25 shorter events, 0.1 us)
Async XLA Ops:
  0.6 10.5 %copy-start = (bf16[128,4096]{1,0:T(8,128)(2,1)S(1)}, bf16[128,4096]{1,0:T(8,128)(2,1)}, u32[]{:S(2)}) copy-start(bf16[128,4096]{1,0:T(8,128)(2,1)} %param.7) | copy-start | bytes 3145732
  1.7 10.1 %copy-start.5 = (bf16[16,4096]{1,0:T(8,128)(2,1)}, bf16[16,4096]{1,0:T(8,128)(2,1)S(1)}, u32[]{:S(2)}) copy-start(bf16[16,4096]{1,0:T(8,128)(2,1)S(1)} %slice_bitcast_fusion.3.refs_0_) | copy-start | bytes 393220
  1.7 58.6 %collective-permute-start.2 = (bf16[16,4096]{1,0:T(8,128)(2,1)S(1)}, bf16[16,4096]{1,0:T(8,128)(2,1)S(1)}, u32[]{:S(2)}, u32[]{:S(2)}) collective-permute-start(bf16[16,4096]{1,0:T(8,128)(2,1)S(1)} %slice_bitcast_fusion.3.refs_0_), channel_id=1, source_target_pairs={{0,1}} | collective-permute-start | bytes 393224 | tf_op jit(solution)/shard_map/ppermute | solution.py:266
  4.1 208.0 %collective-permute-start.7 = (bf16[16,4096]{1,0:T(8,128)(2,1)S(1)}, bf16[16,4096]{1,0:T(8,128)(2,1)S(1)}, u32[]{:S(2)}, u32[]{:S(2)}) collective-permute-start(bf16[16,4096]{1,0:T(8,128)(2,1)S(1)} %slice_bitcast_fusion.3.refs_0_), channel_id=1, source_target_pairs={{1,17},{2,18},{3,19},{4,20},{5,21},{6,22},{7,23},{8,24},{9,25},{10... | collective-permute-start | bytes 393224 | tf_op jit(solution)/shard_map/ppermute | solution.py:280
  4.8 82.6 %collective-permute-start = (bf16[448,4096]{1,0:T(8,128)(2,1)}, bf16[448,4096]{1,0:T(8,128)(2,1)}, u32[]{:S(2)}, u32[]{:S(2)}) collective-permute-start(bf16[448,4096]{1,0:T(8,128)(2,1)} %bitcast.51), channel_id=1, source_target_pairs={{0,16},{16,0},{1,17},{17,1},{2,18},{18,2},{3,19},{19,3},{4,20},{20... | collective-permute-start | bytes 11010056 | tf_op jit(solution)/shard_map/ppermute | solution.py:35
  50.7 9.5 %copy-start.3 = (bf16[128,448]{0,1:T(8,128)(2,1)S(1)}, bf16[128,448]{0,1:T(8,128)(2,1)}, u32[]{:S(2)}) copy-start(bf16[128,448]{0,1:T(8,128)(2,1)} %param.6) | copy-start | bytes 344068
  50.7 46.6 %collective-permute-start.1 = (bf16[16,512]{1,0:T(8,128)(2,1)}, bf16[16,512]{1,0:T(8,128)(2,1)S(1)}, u32[]{:S(2)}, u32[]{:S(2)}) collective-permute-start(bf16[16,512]{1,0:T(8,128)(2,1)} %get-tuple-element.9), channel_id=1, source_target_pairs={{17,1},{19,3},{21,5},{23,7},{25,9},{27,11},{29,13},{31,15}} | collective-permute-start | bytes 49160 | tf_op jit(solution)/shard_map/ppermute | solution.py:268
  55.0 149.3 %collective-permute-start.4 = (bf16[320,4096]{1,0:T(8,128)(2,1)}, bf16[320,4096]{1,0:T(8,128)(2,1)}, u32[]{:S(2)}, u32[]{:S(2)}) collective-permute-start(bf16[320,4096]{1,0:T(8,128)(2,1)} %slice_bitcast_fusion), channel_id=1, source_target_pairs={{0,16},{16,0},{1,17},{17,1},{2,18},{18,2},{3,19},{19,3},{4,20},{20... | collective-permute-start | bytes 7864328 | tf_op jit(solution)/shard_map/ppermute | solution.py:35
  60.3 148.8 %collective-permute-start.5 = (bf16[88,4096]{1,0:T(8,128)(2,1)}, bf16[88,4096]{1,0:T(8,128)(2,1)}, u32[]{:S(2)}, u32[]{:S(2)}) collective-permute-start(bf16[88,4096]{1,0:T(8,128)(2,1)} %slice_bitcast_fusion.1), channel_id=1, source_target_pairs={{0,16},{16,0},{1,17},{17,1},{2,18},{18,2},{3,19},{19,3},{4,20},{20... | collective-permute-start | bytes 2162696 | tf_op jit(solution)/shard_map/ppermute | solution.py:35
  87.3 11.8 %collective-permute-start.3 = (bf16[16,4096]{1,0:T(8,128)(2,1)S(1)}, bf16[16,4096]{1,0:T(8,128)(2,1)S(1)}, u32[]{:S(2)}, u32[]{:S(2)}) collective-permute-start(bf16[16,4096]{1,0:T(8,128)(2,1)S(1)} %collective-permute-done.2), channel_id=1, source_target_pairs={{1,16}} | collective-permute-start | bytes 393224 | tf_op jit(solution)/shard_map/ppermute | solution.py:267
  94.8 2.5 %copy-start.2 = (bf16[448,4096]{1,0:T(8,128)(2,1)}, bf16[448,4096]{1,0:T(8,128)(2,1)S(1)}, u32[]{:S(2)}) copy-start(bf16[448,4096]{1,0:T(8,128)(2,1)S(1)} %fusion.2) | copy-start | bytes 11010052
  94.8 103.1 %copy-start.4 = (bf16[4,2,2,8,4096]{4,3,2,1,0:T(8,128)(2,1)S(1)}, bf16[4,2,2,8,4096]{4,3,2,1,0:T(8,128)(2,1)}, u32[]{:S(2)}) copy-start(bf16[4,2,2,8,4096]{4,3,2,1,0:T(8,128)(2,1)} %get-tuple-element.11) | copy-start | bytes 3145732
  97.3 1.9 copy-start.8
  97.3 114.0 %collective-permute-start.6 = (bf16[24,4096]{1,0:T(8,128)(2,1)S(1)}, bf16[24,4096]{1,0:T(8,128)(2,1)S(1)}, u32[]{:S(2)}, u32[]{:S(2)}) collective-permute-start(bf16[24,4096]{1,0:T(8,128)(2,1)S(1)} %slice_bitcast_fusion.2), channel_id=1, source_target_pairs={{0,16},{16,0},{1,17},{17,1},{2,18},{18,2},{3,19},{19,3},{4,20},{20... | collective-permute-start | bytes 589832 | tf_op jit(solution)/shard_map/ppermute | solution.py:35
  99.2 0.7 copy-start.6
  201.4 2.9 %copy-start.1 = (f32[448,4096]{1,0:T(8,128)}, f32[448,4096]{1,0:T(8,128)S(1)}, u32[]{:S(2)}) copy-start(f32[448,4096]{1,0:T(8,128)S(1)} %fusion.4.base_ref) | copy-start | bytes 22020100
  204.4 4.8 %slice-start = ((f32[448,4096]{1,0:T(8,128)}), f32[88,4096]{1,0:T(8,128)S(1)}, s32[]{:S(2)}) async-start(f32[448,4096]{1,0:T(8,128)} %copy-done.1), calls=%async_computation | async-start | bytes 2883584 | tf_op jit(solution)/shard_map/slice | solution.py:295
  204.4 7.0 %slice-start.1 = ((f32[448,4096]{1,0:T(8,128)}), f32[24,4096]{1,0:T(8,128)S(1)}, s32[]{:S(2)}) async-start(f32[448,4096]{1,0:T(8,128)} %copy-done.1), calls=%async_computation.1 | async-start | bytes 786432 | tf_op jit(solution)/shard_map/slice | solution.py:295
  209.1 3.0 %slice-start.2 = ((f32[448,4096]{1,0:T(8,128)}), f32[16,4096]{1,0:T(8,128)S(1)}, s32[]{:S(2)}) async-start(f32[448,4096]{1,0:T(8,128)} %copy-done.1), calls=%async_computation.2 | async-start | bytes 524288 | tf_op jit(solution)/shard_map/slice | solution.py:295
  209.1 3.0 %copy-start.7 = (bf16[16,4096]{1,0:T(8,128)(2,1)S(1)}, bf16[16,4096]{1,0:T(8,128)(2,1)}, u32[]{:S(2)}) copy-start(bf16[16,4096]{1,0:T(8,128)(2,1)} %get-tuple-element.15) | copy-start | bytes 393220
